TPU v7x, 32 devices: a whole 2x2x4 slice. The times are simulated.
32 devices in a mesh: mesh: 4 (over y, x), sub: 8 (over z, core).
Axes of the slice: x: 2, y: 2, z: 4, core: 2. Of those that a mesh axis runs over, the one named last changes fastest.
Arguments:
- displacement: float32 [3, 2, 32, 1024], P(None, None, 'mesh', 'sub'), may hold values from -4 to 4
- velocity: float32 [3, 2, 32, 1024], P(None, None, 'mesh', 'sub'), may hold values from -6 to 6
- node_mass: float32 [2, 32, 1024], P(None, 'mesh', 'sub'), may hold values from 0.5 to 2
- moduli: float32 [2, 32, 1024], P(None, 'mesh', 'sub'), may hold values from 0.5 to 2
- stiffness: float32 [24, 24], replicated, may hold values from -0.45 to 12, as said below
- surface_ref: float32 [3, 32, 1024], P(None, 'mesh', 'sub'), may hold values from -6 to 6
- facets: float32 [4, 8, 6, 1024], P('mesh', 'sub'), may hold values from -6 to 6
- penalty: float32 [4, 8, 1024], P('mesh', 'sub'), may hold values from 0.5 to 4
- owners: int32 [2, 4, 8, 8, 1], P(None, 'mesh', 'sub'), may hold values from 0 to 3; in each aligned block of 8 rows (0 to 7, 8 to 15, ..., all dimensions but the last counted through in order) at most 4 rows name the same one
- facet_pairs: int32 [2, 32, 1024], P(None, 'mesh', 'sub'), may hold values from 0 to 1023
Outputs:
- final_displacement: float32 [3, 2, 32, 1024], P(None, None, 'mesh', 'sub')
- final_velocity: float32 [3, 2, 32, 1024], P(None, None, 'mesh', 'sub')
Inputs may be any that keep to these rules, and one draw needn't show every extreme that they name: `owners`: in every step no device sends more than 4 of its blocks to one owner, and some device sends exactly 4 to one owner. `stiffness`: Symmetric.
All inputs are finite; a program needn't handle non-finite values.
Results may differ from a plain program's by a relative error of at most 0.0001.
Values sent between devices are 32-bit elements; how exact they have to be, the bound alone decides.
A program may use at most 64 MiB of HBM per device.

v0:
```python
import functools

import jax
import jax.numpy as jnp
from jax import lax
from jax.experimental import pallas as pl
from jax.experimental.pallas import tpu as pltpu
from jax.sharding import PartitionSpec as P

TIME_STEP = 0.1
MESH = pl.DeviceIdType.MESH
ROWS = 8
LANES = 128
DIRECTIONS = ((1, 1), (1, -1), (-1, 1), (-1, -1), (1, 0), (-1, 0), (0, 1), (0, -1))
SLOT = {d: i for i, d in enumerate(DIRECTIONS)}
PAD = 24


def kernel(
    n_mesh,
    n_sub,
    steps,
    stiff_hbm,
    owners_hbm,
    disp_hbm,
    vel_hbm,
    mass_hbm,
    moduli_hbm,
    surf_hbm,
    facets_hbm,
    penalty_hbm,
    pairs_hbm,
    out_disp,
    out_vel,
    stiff,
    owners,
    own,
    vel,
    mass,
    surf,
    pairs,
    table,
    packed,
    arrived,
    wide,
    found,
    local_sem,
    table_send,
    table_recv,
    halo_send,
    halo_recv,
):
    q, s = lax.axis_index("mesh"), lax.axis_index("sub")

    def at(dq, ds):
        return (lax.rem(q + dq + n_mesh, n_mesh), lax.rem(s + ds + n_sub, n_sub))

    chunks = table.shape[1] // 8
    copies = [
        pltpu.make_async_copy(src, dst, local_sem.at[i])
        for i, (src, dst) in enumerate(
            (
                (disp_hbm, own.at[pl.ds(0, 48)]),
                (moduli_hbm, own.at[pl.ds(48, 16)]),
                (facets_hbm, table.at[q, pl.ds(0, 6 * chunks)]),
                (penalty_hbm, table.at[q, pl.ds(6 * chunks, chunks)]),
                (pairs_hbm, pairs),
                (surf_hbm, surf),
                (vel_hbm, vel),
                (mass_hbm, mass),
                (stiff_hbm, stiff),
                (owners_hbm, owners),
            )
        )
    ]
    barrier = pltpu.get_barrier_semaphore()
    partners = [at(*d) for d in DIRECTIONS if d[1] != 0] + [at(d, 0) for d in range(1, n_mesh)]
    for device in partners:
        pl.semaphore_signal(barrier, inc=1, device_id=device, device_id_type=MESH)
    for copy in copies:
        copy.start()

    lane = lax.broadcasted_iota(jnp.int32, (ROWS, LANES), 1)

    def pack(step, planes, count):
        left = jnp.zeros((ROWS, LANES), jnp.float32)
        right = left
        for p in range(count):
            plane = planes[p]
            left = jnp.where(lane == p, pltpu.roll(plane, p, 1) if p else plane, left)
            right = jnp.where(lane == p, pltpu.roll(plane, p + 1, 1), right)
        packed[step, 0] = left
        packed[step, 1] = right

    def pack_rows(step):
        packed[step, 2] = own[pl.ds(0, 8, stride=8), :]
        packed[step, 3] = own[pl.ds(7, 8, stride=8), :]

    def halo(step):
        made = []
        for i, (dq, ds) in enumerate(DIRECTIONS):
            source = (2 if dq < 0 else 3) if dq else (0 if ds < 0 else 1)
            made.append(
                pltpu.make_async_remote_copy(
                    src_ref=packed.at[step, source],
                    dst_ref=arrived.at[step, i],
                    send_sem=halo_send.at[step, i],
                    recv_sem=halo_recv.at[step, i],
                    device_id=at(dq, ds),
                    device_id_type=MESH,
                )
            )
        return made

    for o in range(n_mesh):
        table[o, pl.ds(7 * chunks, chunks), :] = jnp.zeros((chunks, LANES), jnp.float32)
    copies[0].wait()
    copies[1].wait()
    pack_rows(0)
    pack(0, [own[pl.ds(8 * p, 8), :] for p in range(8)], 8)
    pl.semaphore_wait(barrier, len(partners))
    halos = halo(0)
    for copy in halos:
        copy.start()
    copies[2].wait()
    copies[3].wait()
    shared = []
    for d in range(1, n_mesh):
        used = table.at[q, pl.ds(0, 7 * chunks)]
        shared.append(
            pltpu.make_async_remote_copy(
                src_ref=used,
                dst_ref=used,
                send_sem=table_send.at[d - 1],
                recv_sem=table_recv.at[d - 1],
                device_id=at(d, 0),
                device_id_type=MESH,
            )
        )
    for copy in shared:
        copy.start()
    for copy in copies[4:]:
        copy.wait()
    inverse = [TIME_STEP / mass[pl.ds(8 * a, 8), :] for a in range(2)]

    def gather(step):
        for b in range(ROWS):
            owner = owners[step, b]
            index = jnp.broadcast_to(pairs[pl.ds(step * ROWS + b, 1), :], (ROWS, LANES))
            chunk, place = index >> 7, index & 127
            total = jnp.zeros((ROWS, LANES), jnp.float32)
            for k in range(chunks):
                rows = table[owner, pl.ds(k, 8, stride=chunks), :]
                picked = jnp.take_along_axis(rows, place, axis=1, mode="promise_in_bounds")
                total = jnp.where(chunk == k, picked, total)
            found[step, pl.ds(8 * b, 8), :] = total

    def spread_middle(step, planes, count):
        for p in range(count):
            wide[1, pl.ds(p * PAD + 8, 8), :] = planes[p]
        for dq, row in ((1, 7), (-1, 16)):
            wide[1, pl.ds(row, 8, stride=PAD), :] = arrived[step, SLOT[(dq, 0)]]

    def spread_sides(step, turned, count):
        from_left, from_right = arrived[step, SLOT[(0, 1)]], arrived[step, SLOT[(0, -1)]]
        for p in range(count):
            before = pltpu.roll(from_left, LANES - p, 1) if p else from_left
            after = pltpu.roll(from_right, LANES - 1 - p, 1)
            rows = pl.ds(p * PAD + 8, 8)
            wide[0, rows, :] = jnp.where(lane == 0, before, turned[p][0])
            wide[2, rows, :] = jnp.where(lane == LANES - 1, after, turned[p][1])
        for dq, row in ((1, 7), (-1, 16)):
            centre = arrived[step, SLOT[(dq, 0)]]
            west, east = arrived[step, SLOT[(dq, 1)]], arrived[step, SLOT[(dq, -1)]]
            rows = pl.ds(row, 8, stride=PAD)
            wide[0, rows, :] = pltpu.roll(jnp.where(lane == LANES - 1, west, centre), 1, 1)
            wide[2, rows, :] = pltpu.roll(jnp.where(lane == 0, east, centre), LANES - 1, 1)

    def shifted(p, di, dj):
        return wide[dj + 1, pl.ds(p * PAD + 8 + di, 8), :]

    scales = {}
    planes = [own[pl.ds(8 * p, 8), :] for p in range(8)]
    for step in range(steps):
        if step == 0:
            for copy in shared:
                copy.wait_recv()
        gather(step)
        facet = [found[step, pl.ds(c, 8, stride=8), :] for c in range(7)]
        points = [surf[pl.ds(8 * m, 8), :] + planes[2 * m] for m in range(3)]
        gap = sum(facet[3 + m] * (points[m] - facet[m]) for m in range(3))
        strength = facet[6] * jnp.maximum(-gap, 0.0)
        push = [facet[3 + m] * strength for m in range(3)]
        count = 8 if step == 0 else 6
        turned = [(pltpu.roll(p, 1, 1), pltpu.roll(p, LANES - 1, 1)) for p in planes[:count]]
        sums = {(b, e): [None] * 6 for b in (0, 1) for e in (0, 1)}

        def accumulate(middle):
            for b, e in sums:
                for corner in range(8):
                    a2, b2, e2 = corner >> 2, (corner >> 1) & 1, corner & 1
                    if (e2 == e) != middle:
                        continue
                    for m2 in range(3):
                        value = shifted(2 * m2 + a2, b2 - b, e2 - e)
                        for o in range(6):
                            row = 3 * (4 * (o % 2) + 2 * b + e) + o // 2
                            term = stiff[row, 3 * corner + m2] * value
                            before = sums[b, e][o]
                            sums[b, e][o] = term if before is None else before + term

        for d in ((1, 0), (-1, 0)):
            halos[SLOT[d]].wait_recv()
        spread_middle(step, planes, count)
        accumulate(True)
        for d in DIRECTIONS:
            if d[1] != 0:
                halos[SLOT[d]].wait_recv()
        spread_sides(step, turned, count)
        if step == 0:
            both = {
                (di, dj): shifted(6, di, dj) + shifted(7, di, dj) for di in (-1, 0, 1) for dj in (-1, 0, 1)
            }
            for b in (0, 1):
                for e in (0, 1):
                    scales[b, e] = 0.125 * (
                        (both[-b, -e] + both[-b, 1 - e]) + (both[1 - b, -e] + both[1 - b, 1 - e])
                    )
        accumulate(False)
        force = [None] * 6
        for b, e in sums:
            for o in range(6):
                term = scales[b, e] * sums[b, e][o]
                force[o] = term if force[o] is None else force[o] + term
        last = step == steps - 1
        fresh = []
        for o in range(6):
            m, a = o // 2, o % 2
            net = push[m] - force[o] if a == 0 else -force[o]
            rows = pl.ds(8 * o, 8)
            speed = vel[rows, :] + inverse[a] * net
            moved = planes[o] + TIME_STEP * speed
            fresh.append(moved)
            if last:
                out_vel[rows, :] = speed
                out_disp[rows, :] = moved
            else:
                vel[rows, :] = speed
                own[rows, :] = moved
        planes = fresh
        sent = halos
        if not last:
            halos = halo(step + 1)
            pack_rows(step + 1)
            for d in DIRECTIONS:
                if d[0] != 0:
                    halos[SLOT[d]].start()
            pack(step + 1, planes, 6)
            for d in DIRECTIONS:
                if d[0] == 0:
                    halos[SLOT[d]].start()
        for copy in sent:
            copy.wait_send()
    for copy in shared:
        copy.wait_send()


def flush(moved, speed, out_moved, out_speed, sem):
    copies = [
        pltpu.make_async_copy(src, dst, sem.at[i])
        for i, (src, dst) in enumerate(((moved, out_moved), (speed, out_speed)))
    ]
    for copy in copies:
        copy.start()
    for copy in copies:
        copy.wait()


def shards(
    displacement,
    velocity,
    node_mass,
    moduli,
    stiffness,
    surface_ref,
    facets,
    penalty,
    owners,
    facet_pairs,
):
    steps = owners.shape[0]
    width = facets.shape[3]
    n_mesh, n_sub = lax.axis_size("mesh"), lax.axis_size("sub")
    assert displacement.shape == (3, 2, ROWS, LANES)
    f32 = jnp.float32
    out = pltpu.VMEM((6 * ROWS, LANES), f32)
    anywhere = pl.BlockSpec(memory_space=pl.ANY)
    vmem = pl.BlockSpec(memory_space=pltpu.VMEM)
    dma = pltpu.SemaphoreType.DMA
    moved, speed = pl.pallas_call(
        functools.partial(kernel, n_mesh, n_sub, steps),
        out_shape=(out, out),
        in_specs=[anywhere] * 10,
        out_specs=(vmem, vmem),
        scratch_shapes=[
            pltpu.SMEM((24, 24), f32),
            pltpu.SMEM((steps, ROWS), jnp.int32),
            pltpu.VMEM((8 * ROWS, LANES), f32),
            pltpu.VMEM((6 * ROWS, LANES), f32),
            pltpu.VMEM((2 * ROWS, LANES), f32),
            pltpu.VMEM((3 * ROWS, LANES), f32),
            pltpu.VMEM((steps * ROWS, LANES), jnp.int32),
            pltpu.VMEM((n_mesh, 8 * width // LANES, LANES), f32),
            pltpu.VMEM((steps, 4, ROWS, LANES), f32),
            pltpu.VMEM((steps, 8, ROWS, LANES), f32),
            pltpu.VMEM((3, 8 * PAD, LANES), f32),
            pltpu.VMEM((steps, 8 * ROWS, LANES), f32),
            dma((10,)),
            dma((n_mesh - 1,)),
            dma((n_mesh - 1,)),
            dma((steps, 8)),
            dma((steps, 8)),
        ],
        compiler_params=pltpu.CompilerParams(collective_id=0, has_side_effects=True),
    )(
        stiffness,
        owners.reshape(steps, ROWS),
        displacement.reshape(6 * ROWS, LANES),
        velocity.reshape(6 * ROWS, LANES),
        node_mass.reshape(2 * ROWS, LANES),
        moduli.reshape(2 * ROWS, LANES),
        surface_ref.reshape(3 * ROWS, LANES),
        facets.transpose(0, 2, 1, 3).reshape(6 * width // LANES, LANES),
        penalty.reshape(width // LANES, LANES),
        facet_pairs.reshape(steps * ROWS, LANES),
    )
    moved, speed = pl.pallas_call(
        flush,
        out_shape=[jax.ShapeDtypeStruct((6 * ROWS, LANES), f32)] * 2,
        in_specs=[anywhere, anywhere],
        out_specs=[anywhere, anywhere],
        scratch_shapes=[dma((2,))],
        compiler_params=pltpu.CompilerParams(vmem_limit_bytes=1 << 20),
    )(pltpu.with_memory_space_constraint(moved, pltpu.VMEM), pltpu.with_memory_space_constraint(speed, pltpu.VMEM))
    return moved.reshape(displacement.shape), speed.reshape(velocity.shape)


def solution(mesh):
    in_specs = (
        P(None, None, "mesh", "sub"),
        P(None, None, "mesh", "sub"),
        P(None, "mesh", "sub"),
        P(None, "mesh", "sub"),
        P(),
        P(None, "mesh", "sub"),
        P("mesh", "sub", None, None),
        P("mesh", "sub", None),
        P(None, "mesh", "sub", None, None),
        P(None, "mesh", "sub"),
    )
    out_specs = (P(None, None, "mesh", "sub"), P(None, None, "mesh", "sub"))
    return jax.shard_map(shards, mesh=mesh, in_specs=in_specs, out_specs=out_specs, check_vma=False)
```

profile of v0, /device:TPU:0, one launch (start us, length us, event | category | flops | bytes accessed | tf_op | source)
XLA Modules:
  0.0 16.5 jit_solution(5346885881499778514)
XLA Ops:
  0.6 15.3 %shard_map.113 = (f32[48,128]{1,0:T(8,128)S(1)}, f32[48,128]{1,0:T(8,128)S(1)}) custom-call(f32[24,24]{1,0:T(8,128)} %stiff_hbm.1, s32[2,8]{1,0:T(2,128)} %bitcast.19, f32[48,128]{1,0:T(8,128)} %bitcast.11, f32[48,128]{1,0:T(8,128)} %bitcast.12, f32[16,128]{1,0:T(8,128)} %bitcast.15, f32[16,128]{1,0:T(8,128)} %bitcast.16, f32[24,128]{1,0:T(8,128)} %bitcast.14, ...), custom_call_target="tpu_custom_call" | custom-call | tf_op jit(solution)/shard_map/pallas_call | solution.py:300
  15.9 0.6 %shard_map.114 = (f32[48,128]{1,0:T(8,128)}, f32[48,128]{1,0:T(8,128)}) custom-call(f32[48,128]{1,0:T(8,128)S(1)} %get-tuple-element.6.moved, f32[48,128]{1,0:T(8,128)S(1)} %get-tuple-element.7.speed), custom_call_target="tpu_custom_call" | custom-call | tf_op jit(solution)/shard_map/pallas_call | solution.py:337
where the time goes:
time: 16.7 us; the launch traced here: 16.5 us
  Pallas kernels  15.9 us (95%)
  between operations  0.64 us (4%)
    pallas_call x1, Pallas kernels, shards(): pl.pallas_call(functools.partial(kernel, n_mesh, n_sub, steps), out_shape...  15.3 us
    pallas_call x1, Pallas kernels, shards(): pl.pallas_call(flush, out_shape=[jax.ShapeDtypeStruct((6 * ROWS, LANES),...  0.64 us

commit v1 on v0

v1 whole, which is shorter than its diff:
```python
import functools

import jax
import jax.numpy as jnp
from jax import lax
from jax.experimental import pallas as pl
from jax.experimental.pallas import tpu as pltpu
from jax.sharding import PartitionSpec as P

TIME_STEP = 0.1
MESH = pl.DeviceIdType.MESH
ROWS = 8
LANES = 128
GROUP = 8
GROUPS = LANES // GROUP
F32 = jnp.float32
BF16 = jnp.bfloat16
BLOCKS = 9 * 8
DEPTH = BLOCKS + 8
NEAR = [(dq, ds) for dq in (-1, 0, 1) for ds in (-1, 0, 1) if dq or ds]


def roll(x, shift):
    shift %= LANES
    return pltpu.roll(x, shift, 1) if shift else x


def iota(shape, axis):
    return lax.broadcasted_iota(jnp.int32, shape, axis)


def one_hot(condition):
    return jnp.where(condition, 1.0, 0.0).astype(BF16)


def coefficients(stiff):
    high = stiff.astype(BF16)
    low = (stiff - high.astype(F32)).astype(BF16)
    row = iota((32, 24), 0)
    o, b, e = row & 7, row >> 4, (row >> 3) & 1
    wanted = 3 * (4 * (o & 1) + 2 * b + e) + (o >> 1)
    pick = one_hot((wanted == iota((32, 24), 1)) & (o < 6))
    high = jnp.dot(pick, high, preferred_element_type=F32).astype(BF16)
    low = jnp.dot(pick, low, preferred_element_type=F32).astype(BF16)

    def columns(shape):
        col = iota(shape, 1)
        third = jnp.where(col >= DEPTH, 1, 0) + jnp.where(col >= 2 * DEPTH, 1, 0) + jnp.where(col >= 3 * DEPTH, 1, 0)
        rest = col - DEPTH * third
        off, p = rest >> 3, rest & 7
        di = jnp.where(off >= 3, 1, 0) + jnp.where(off >= 6, 1, 0) - 1
        dj = off - 3 * (di + 1) - 1
        return third, di, dj, p, off < 9

    def inside(b2, e2):
        return (b2 >= 0) & (b2 <= 1) & (e2 >= 0) & (e2 <= 1)

    third, di, dj, p, used = columns((24, 256))
    force = None
    for group in range(4):
        b2, e2 = di + (group >> 1), dj + (group & 1)
        wanted = 3 * (4 * (p & 1) + 2 * b2 + e2) + (p >> 1)
        place = used & inside(b2, e2) & (p < 6) & (wanted == iota((24, 256), 0))
        term = jnp.dot(high, one_hot(place & (third < 2)), preferred_element_type=F32)
        term = term + jnp.dot(low, one_hot(place & (third == 2)), preferred_element_type=F32)
        force = term if force is None else jnp.where((iota((32, 256), 0) >> 3) == group, term, force)
    third, di, dj, p, used = columns((32, 256))
    row = iota((32, 256), 0)
    counted = used & inside(di + (row >> 4), dj + ((row >> 3) & 1)) & (p >= 6) & (third < 2)
    return jnp.concatenate([force, jnp.where(counted, 0.125, 0.0)], axis=0).astype(BF16)


def stacked(blocks):
    x = jnp.concatenate(blocks + [jnp.zeros_like(blocks[0])], axis=0)
    high = x.astype(BF16)
    low = (x - high.astype(F32)).astype(BF16)
    return jnp.concatenate([high, low, high, jnp.zeros((256 - 3 * DEPTH, x.shape[1]), BF16)], axis=0)


def kernel(
    n_mesh,
    n_sub,
    width,
    stiff_hbm,
    owners_hbm,
    disp_hbm,
    vel_hbm,
    mass_hbm,
    moduli_hbm,
    surf_hbm,
    facets_hbm,
    penalty_hbm,
    pairs_hbm,
    out_disp,
    out_vel,
    stiff,
    owners,
    own,
    vel,
    mass,
    inverse,
    base,
    pairs,
    raw,
    tables,
    distant,
    edge,
    border,
    edges,
    borders,
    local_sem,
    table_send,
    table_recv,
    edge_send,
    edge_recv,
    border_send,
    border_recv,
):
    q, s = lax.axis_index("mesh"), lax.axis_index("sub")
    chunks = width // LANES
    half = chunks // 2
    bits = width.bit_length() - 1

    def at(dq, ds):
        return (lax.rem(q + dq + n_mesh, n_mesh), lax.rem(s + ds + n_sub, n_sub))

    copies = [
        pltpu.make_async_copy(src, dst, local_sem.at[i])
        for i, (src, dst) in enumerate(
            [
                (disp_hbm, own.at[pl.ds(0, 48)]),
                (moduli_hbm, own.at[pl.ds(48, 16)]),
                (owners_hbm, owners),
                (pairs_hbm, pairs),
                (vel_hbm, vel.at[pl.ds(0, 48)]),
                (mass_hbm, mass),
            ]
            + [(surf_hbm.at[pl.ds(8 * m, 8)], base.at[pl.ds(16 * m, 8)]) for m in range(3)]
            + [
                (facets_hbm, raw.at[pl.ds(0, 6 * chunks)]),
                (penalty_hbm, raw.at[pl.ds(6 * chunks, chunks)]),
                (stiff_hbm, stiff),
            ]
        )
    ]
    for copy in copies:
        copy.start()
    barrier = pltpu.get_barrier_semaphore()
    partners = [(dq, ds) for ds in (0, -1, 1) for dq in range(n_mesh) if dq or ds]
    for device in partners:
        pl.semaphore_signal(barrier, inc=1, device_id=at(*device), device_id_type=MESH)

    lane = iota((8, LANES), 1)
    plane = iota((8, LANES), 0)
    group = lane >> 3
    place_in = lane & 7
    entry = plane < 6
    surface = entry & ((plane & 1) == 0)
    flat = jnp.zeros((8, LANES), F32)
    for p in (1, 3, 5):
        base[pl.ds(8 * p, 8), :] = flat
    base[pl.ds(48, 8), :] = flat - 1.0

    for copy in copies[:9]:
        copy.wait()

    for a in range(2):
        slowness = TIME_STEP / mass[pl.ds(8 * a, 8), :]
        for p in range(a, 8, 2):
            inverse[pl.ds(8 * p, 8), :] = slowness
    holder = jnp.zeros((8, LANES), jnp.int32)
    for b in range(ROWS):
        holder = jnp.where(plane == b, owners[0, b], holder)
    base[pl.ds(56, 8), :] = ((holder << bits) + pairs[pl.ds(0, 8), :]).astype(F32)

    def of_row(ref, i):
        return ref[pl.ds(i, 8, stride=8), :]

    here = {i: of_row(own, i) for i in range(ROWS)}
    gain = {i: of_row(inverse, i) for i in range(ROWS)}
    speed = {i: jnp.where(entry, of_row(vel, i), gain[i]) for i in range(ROWS)}
    point = {i: of_row(base, i) for i in range(ROWS)}
    point = {i: jnp.where(surface, point[i] + here[i], point[i]) for i in range(ROWS)}

    sent = flat
    for g, i in [(i, i) for i in range(ROWS)] + [(8, 0), (9, 1), (14, 6), (15, 7)]:
        deep = roll(here[i], GROUP * g + 4)
        deep = jnp.where(place_in < 2, roll(point[i], GROUP * g + 1), deep)
        deep = jnp.where(place_in > 5, roll(speed[i], GROUP * g + 7), deep)
        sent = jnp.where(group == g, deep, sent)
    edge[...] = sent
    for k, ids in enumerate(((6, 7, 7, 7), (0, 1, 0, 0))):
        for j, (what, i) in enumerate(zip((here, here, speed, point), ids)):
            border[k, pl.ds(8 * j, 8), :] = what[i]

    copies[9].wait()
    copies[10].wait()
    parts = [raw[pl.ds(chunks * c, chunks), :] for c in range(7)]
    root = jnp.sqrt(parts[6])
    normal = [root * parts[3 + m] for m in range(3)]
    offset = normal[0] * parts[0] + normal[1] * parts[1] + normal[2] * parts[2]
    for c, values in enumerate(normal + [offset]):
        for h in range(2):
            tables[q, pl.ds(2 * c + h, half, stride=8), :] = values[half * h : half * (h + 1)]

    pl.semaphore_wait(barrier, len(partners))

    edge_copies = {}
    for i, (dq, ds) in enumerate(NEAR):
        edge_copies[dq, ds] = pltpu.make_async_remote_copy(
            src_ref=edge,
            dst_ref=edges.at[i],
            send_sem=edge_send.at[i],
            recv_sem=edge_recv.at[i],
            device_id=at(-dq, -ds),
            device_id_type=MESH,
        )
    border_copies = [
        pltpu.make_async_remote_copy(
            src_ref=border.at[k],
            dst_ref=borders.at[k],
            send_sem=border_send.at[k],
            recv_sem=border_recv.at[k],
            device_id=at(dq, 0),
            device_id_type=MESH,
        )
        for k, dq in enumerate((1, -1))
    ]
    table_copies = {}
    for i, (dq, ds) in enumerate(partners):
        table_copies[dq, ds] = pltpu.make_async_remote_copy(
            src_ref=tables.at[q],
            dst_ref={0: tables.at[q], 1: distant.at[q], -1: distant.at[n_mesh + q]}[ds],
            send_sem=table_send.at[i],
            recv_sem=table_recv.at[i],
            device_id=at(dq, ds),
            device_id_type=MESH,
        )
    for copy in edge_copies.values():
        copy.start()
    for copy in border_copies:
        copy.start()
    for copy in table_copies.values():
        copy.start()

    copies[11].wait()
    weights = coefficients(stiff[...])

    def elastic(first, second):
        blocks = [jnp.concatenate([a, b], axis=1) for a, b in zip(first, second)]
        got = jnp.dot(weights, stacked(blocks), preferred_element_type=F32)
        terms = [got[8 * g : 8 * g + 8] * got[32 + 8 * g : 40 + 8 * g] for g in range(4)]
        force = (terms[0] + terms[1]) + (terms[2] + terms[3])
        return force[:, :LANES], force[:, LANES:]

    def around(rows, i):
        return [x for di in (-1, 0, 1) for x in rows[i + di]]

    def turned(x):
        return (roll(x, 1), x, roll(x, -1))

    def narrowed(total, second):
        return jnp.where(second, pltpu.roll(total, 7, 0), total)

    def facet_of(step, i):
        index = jnp.broadcast_to(pairs[pl.ds(step * ROWS + i, 1), :], (8, LANES))
        chunk, place = index >> 7, index & (LANES - 1)
        second = chunk >= half
        chunk = jnp.where(second, chunk - half, chunk)
        owner = owners[step, i]
        total = flat
        for k in range(half):
            picked = jnp.take_along_axis(tables[owner, pl.ds(8 * k, 8), :], place, axis=1, mode="promise_in_bounds")
            total = jnp.where(chunk == k, picked, total)
        return narrowed(total, second)

    def facet_by(code, sides, choice):
        code = code.astype(jnp.int32)
        owner, index = code >> bits, code & (width - 1)
        chunk, place = index >> 7, index & (LANES - 1)
        second = chunk >= half
        chunk = jnp.where(second, chunk - half, chunk) + half * owner
        if choice is not None:
            chunk = chunk + choice * (half * n_mesh)
        total = flat
        for side in sides:
            for o in range(n_mesh):
                for k in range(half):
                    ref, at_slot = (distant, (side - 1) * n_mesh + o) if side else (tables, o)
                    rows = ref[at_slot, pl.ds(8 * k, 8), :]
                    picked = jnp.take_along_axis(rows, place, axis=1, mode="promise_in_bounds")
                    total = jnp.where(chunk == (side * n_mesh + o) * half + k, picked, total)
        return narrowed(total, second)

    def push_of(facet, at_point):
        product = jnp.where(surface | (plane == 6), facet * at_point, 0.0)
        product = product + pltpu.roll(product, 4, 0)
        product = product + pltpu.roll(product, 2, 0)
        return jnp.where(surface, facet * jnp.maximum(-product, 0.0), 0.0)

    def ring_step(values, moving, net):
        slow = jnp.where(
            (plane & 1) == 0, jnp.broadcast_to(moving[6:7], (8, LANES)), jnp.broadcast_to(moving[7:8], (8, LANES))
        )
        faster = moving + slow * net
        return jnp.where(entry, values + TIME_STEP * faster, values)

    rows = {i: turned(here[i]) for i in range(ROWS)}
    force = {}
    for i in (1, 3, 5):
        force[i], force[i + 1] = elastic(around(rows, i), around(rows, i + 1))
    for copy in border_copies:
        copy.wait_recv()
    for i, (k, j) in {-2: (0, 0), -1: (0, 1), 8: (1, 0), 9: (1, 1)}.items():
        here[i] = borders[k, pl.ds(8 * j, 8), :]
        rows[i] = turned(here[i])
    force[0], force[7] = elastic(around(rows, 0), around(rows, 7))
    force[-1], force[8] = elastic(around(rows, -1), around(rows, 8))
    for device, copy in table_copies.items():
        if device[1] == 0:
            copy.wait_recv()
    later = {}
    after, fast = {}, {}
    for i in range(ROWS):
        net = push_of(facet_of(0, i), point[i]) - force[i]
        later[i] = facet_of(1, i)
        fast[i] = speed[i] + gain[i] * net
        after[i] = jnp.where(entry, here[i] + TIME_STEP * fast[i], here[i])
    for i, k in ((-1, 0), (8, 1)):
        moving, at_point = borders[k, pl.ds(16, 8), :], borders[k, pl.ds(24, 8), :]
        facet = facet_by(jnp.broadcast_to(at_point[7:8], (8, LANES)), (0,), None)
        after[i] = ring_step(here[i], moving, push_of(facet, at_point) - force[i])
    shifted = {i: (roll(after[i], 1), roll(after[i], -1)) for i in range(-1, 9)}

    for copy in edge_copies.values():
        copy.wait_recv()

    def column(ds):
        middle = sent if ds == 0 else edges[NEAR.index((0, ds))]
        beyond = jnp.where(group < 12, edges[NEAR.index((1, ds))], edges[NEAR.index((-1, ds))])
        return jnp.where(group < 8, middle, beyond)

    left, centre, right = column(-1), column(0), column(1)
    from_before = (place_in == 0) | (place_in == 2) | (place_in == 3) | (place_in == 6)
    strips = [jnp.where(from_before, left, centre), jnp.where(from_before, centre, right)]
    strip_force = elastic(
        *([roll(x, -(GROUP * di + dj)) for di in (-1, 0, 1) for dj in (-1, 0, 1)] for x in strips)
    )
    strip_speed = [roll(x, -3) for x in strips]
    strip_point = [roll(x, 3) for x in strips]
    for device, copy in table_copies.items():
        if device[1] != 0:
            copy.wait_recv()
    strip_after = []
    for k in range(2):
        outer = place_in == (3, 4)[k]
        facet = facet_by(
            jnp.broadcast_to(strip_point[k][7:8], (8, LANES)), (0, 1 + k), jnp.where(outer, 1 + k, 0)
        )
        net = push_of(facet, strip_point[k]) - strip_force[k]
        strip_after.append(ring_step(strips[k], strip_speed[k], net))
    corner = jnp.where(place_in == 4, strip_after[0], strip_after[1])

    rows = {}
    for i in range(-1, 9):
        start = GROUP * (i % GROUPS) + 3
        mid = jnp.where((lane == 0) | (lane == LANES - 1), roll(corner, -(start + 1)), after[i])
        before = jnp.where(lane < 2, roll(strip_after[0], -start), shifted[i][0])
        behind = jnp.where(lane >= LANES - 2, roll(strip_after[1], LANES - 2 - start), shifted[i][1])
        rows[i] = (before, mid, behind)
    for i in range(0, ROWS, 2):
        force[i], force[i + 1] = elastic(around(rows, i), around(rows, i + 1))
    side = (lane == 0) | (lane == LANES - 1)
    for i in range(ROWS):
        mid = rows[i][1]
        at_point = of_row(base, i)
        at_point = jnp.where(surface, at_point + mid, at_point)
        net = push_of(later[i], at_point) - force[i]
        past = jnp.where(side, (mid - here[i]) * (1.0 / TIME_STEP), fast[i])
        past = past + gain[i] * net
        out_vel[pl.ds(i, 6, stride=8), :] = past[0:6]
        out_disp[pl.ds(i, 6, stride=8), :] = (mid + TIME_STEP * past)[0:6]

    for copy in list(edge_copies.values()) + border_copies + list(table_copies.values()):
        copy.wait_send()


def flush(moved, speed, out_moved, out_speed, sem):
    copies = [
        pltpu.make_async_copy(src, dst, sem.at[i])
        for i, (src, dst) in enumerate(((moved, out_moved), (speed, out_speed)))
    ]
    for copy in copies:
        copy.start()
    for copy in copies:
        copy.wait()


def shards(
    displacement,
    velocity,
    node_mass,
    moduli,
    stiffness,
    surface_ref,
    facets,
    penalty,
    owners,
    facet_pairs,
):
    steps = owners.shape[0]
    width = facets.shape[3]
    n_mesh, n_sub = lax.axis_size("mesh"), lax.axis_size("sub")
    assert displacement.shape == (3, 2, ROWS, LANES) and steps == 2
    assert width == 1 << (width.bit_length() - 1) and width >= 2 * LANES
    out = pltpu.VMEM((6 * ROWS, LANES), F32)
    anywhere = pl.BlockSpec(memory_space=pl.ANY)
    vmem = pl.BlockSpec(memory_space=pltpu.VMEM)
    dma = pltpu.SemaphoreType.DMA
    moved, speed = pl.pallas_call(
        functools.partial(kernel, n_mesh, n_sub, width),
        out_shape=(out, out),
        in_specs=[anywhere] * 10,
        out_specs=(vmem, vmem),
        scratch_shapes=[
            pltpu.VMEM((24, 24), F32),
            pltpu.SMEM((steps, ROWS), jnp.int32),
            pltpu.VMEM((8 * ROWS, LANES), F32),
            pltpu.VMEM((8 * ROWS, LANES), F32),
            pltpu.VMEM((2 * ROWS, LANES), F32),
            pltpu.VMEM((8 * ROWS, LANES), F32),
            pltpu.VMEM((8 * ROWS, LANES), F32),
            pltpu.VMEM((steps * ROWS, LANES), jnp.int32),
            pltpu.VMEM((7 * width // LANES, LANES), F32),
            pltpu.VMEM((n_mesh, 4 * width // LANES, LANES), F32),
            pltpu.VMEM((2 * n_mesh, 4 * width // LANES, LANES), F32),
            pltpu.VMEM((8, LANES), F32),
            pltpu.VMEM((2, 32, LANES), F32),
            pltpu.VMEM((8, 8, LANES), F32),
            pltpu.VMEM((2, 32, LANES), F32),
            dma((12,)),
            dma((3 * n_mesh - 1,)),
            dma((3 * n_mesh - 1,)),
            dma((8,)),
            dma((8,)),
            dma((2,)),
            dma((2,)),
        ],
        compiler_params=pltpu.CompilerParams(collective_id=0, has_side_effects=True),
    )(
        stiffness,
        owners.reshape(steps, ROWS),
        displacement.reshape(6 * ROWS, LANES),
        velocity.reshape(6 * ROWS, LANES),
        node_mass.reshape(2 * ROWS, LANES),
        moduli.reshape(2 * ROWS, LANES),
        surface_ref.reshape(3 * ROWS, LANES),
        facets.transpose(0, 2, 1, 3).reshape(6 * width // LANES, LANES),
        penalty.reshape(width // LANES, LANES),
        facet_pairs.reshape(steps * ROWS, LANES),
    )
    moved, speed = pl.pallas_call(
        flush,
        out_shape=[jax.ShapeDtypeStruct((6 * ROWS, LANES), F32)] * 2,
        in_specs=[anywhere, anywhere],
        out_specs=[anywhere, anywhere],
        scratch_shapes=[dma((2,))],
        compiler_params=pltpu.CompilerParams(vmem_limit_bytes=1 << 20),
    )(pltpu.with_memory_space_constraint(moved, pltpu.VMEM), pltpu.with_memory_space_constraint(speed, pltpu.VMEM))
    return moved.reshape(displacement.shape), speed.reshape(velocity.shape)


def solution(mesh):
    in_specs = (
        P(None, None, "mesh", "sub"),
        P(None, None, "mesh", "sub"),
        P(None, "mesh", "sub"),
        P(None, "mesh", "sub"),
        P(),
        P(None, "mesh", "sub"),
        P("mesh", "sub", None, None),
        P("mesh", "sub", None),
        P(None, "mesh", "sub", None, None),
        P(None, "mesh", "sub"),
    )
    out_specs = (P(None, None, "mesh", "sub"), P(None, None, "mesh", "sub"))
    return jax.shard_map(shards, mesh=mesh, in_specs=in_specs, out_specs=out_specs, check_vma=False)
```

time: 16.7 us -> 13 us (0.78)
  Pallas kernels: 15.9 us -> 12.1 us
    pallas_call x1, Pallas kernels: 15.3 us -> 11.5 us  [shards(): pl.pallas_call(functools.partial(kernel, n_mesh, n_sub, width), out_shape...]
where the time goes in v1:
time: 13 us; the launch traced here: 12.8 us
  Pallas kernels  12.1 us (93%)
  between operations  0.64 us (5%)
    pallas_call x1, Pallas kernels, shards(): pl.pallas_call(functools.partial(kernel, n_mesh, n_sub, width), out_shape...  11.5 us
    pallas_call x1, Pallas kernels, shards(): pl.pallas_call(flush, out_shape=[jax.ShapeDtypeStruct((6 * ROWS, LANES),...  0.64 us

profile of v1, /device:TPU:0, one launch (start us, length us, event | category | flops | bytes accessed | tf_op | source)
XLA Modules:
  0.0 12.8 jit_solution(1669669313554851111)
XLA Ops:
  0.6 11.5 %shard_map.113 = (f32[48,128]{1,0:T(8,128)S(1)}, f32[48,128]{1,0:T(8,128)S(1)}) custom-call(f32[24,24]{1,0:T(8,128)} %stiff_hbm.1, s32[2,8]{1,0:T(2,128)} %bitcast.19, f32[48,128]{1,0:T(8,128)} %bitcast.11, f32[48,128]{1,0:T(8,128)} %bitcast.12, f32[16,128]{1,0:T(8,128)} %bitcast.15, f32[16,128]{1,0:T(8,128)} %bitcast.16, f32[24,128]{1,0:T(8,128)} %bitcast.14, ...), custom_call_target="tpu_custom_call" | custom-call | tf_op jit(solution)/shard_map/pallas_call | solution.py:420
  12.2 0.6 %shard_map.114 = (f32[48,128]{1,0:T(8,128)}, f32[48,128]{1,0:T(8,128)}) custom-call(f32[48,128]{1,0:T(8,128)S(1)} %get-tuple-element.6.moved, f32[48,128]{1,0:T(8,128)S(1)} %get-tuple-element.7.speed), custom_call_target="tpu_custom_call" | custom-call | tf_op jit(solution)/shard_map/pallas_call | solution.py:462

commit v2 on v1

--- a/solution.py
+++ b/solution.py
@@ -95,11 +95,8 @@
     out_vel,
     stiff,
     owners,
-    own,
-    vel,
-    mass,
+    inbox,
     inverse,
-    base,
     pairs,
     raw,
     tables,
@@ -108,15 +105,12 @@
     border,
     edges,
     borders,
-    local_sem,
-    table_send,
-    table_recv,
-    edge_send,
-    edge_recv,
-    border_send,
-    border_recv,
+    sems,
+    ready,
 ):
     q, s = lax.axis_index("mesh"), lax.axis_index("sub")
+    own, vel = inbox.at[pl.ds(0, 64)], inbox.at[pl.ds(64, 64)]
+    mass, base = inbox.at[pl.ds(112, 16)], inbox.at[pl.ds(128, 64)]
     chunks = width // LANES
     half = chunks // 2
     bits = width.bit_length() - 1
@@ -124,31 +118,40 @@
     def at(dq, ds):
         return (lax.rem(q + dq + n_mesh, n_mesh), lax.rem(s + ds + n_sub, n_sub))
 
+    def landed(ref, i):
+        return pltpu.make_async_copy(ref, ref, sems.at[i])
+
     copies = [
-        pltpu.make_async_copy(src, dst, local_sem.at[i])
-        for i, (src, dst) in enumerate(
-            [
-                (disp_hbm, own.at[pl.ds(0, 48)]),
-                (moduli_hbm, own.at[pl.ds(48, 16)]),
-                (owners_hbm, owners),
-                (pairs_hbm, pairs),
-                (vel_hbm, vel.at[pl.ds(0, 48)]),
-                (mass_hbm, mass),
-            ]
-            + [(surf_hbm.at[pl.ds(8 * m, 8)], base.at[pl.ds(16 * m, 8)]) for m in range(3)]
-            + [
-                (facets_hbm, raw.at[pl.ds(0, 6 * chunks)]),
-                (penalty_hbm, raw.at[pl.ds(6 * chunks, chunks)]),
-                (stiff_hbm, stiff),
-            ]
-        )
+        pltpu.make_async_copy(src, dst, sems.at[i])
+        for src, dst, i in [
+            (disp_hbm, own.at[pl.ds(0, 48)], 0),
+            (moduli_hbm, own.at[pl.ds(48, 16)], 0),
+            (owners_hbm, owners, 2),
+            (pairs_hbm, pairs, 1),
+            (vel_hbm, vel.at[pl.ds(0, 48)], 0),
+            (mass_hbm, mass, 0),
+        ]
+        + [(surf_hbm.at[pl.ds(8 * m, 8)], base.at[pl.ds(16 * m, 8)], 0) for m in range(3)]
+        + [
+            (facets_hbm, raw.at[pl.ds(0, 6 * chunks)], 3),
+            (penalty_hbm, raw.at[pl.ds(6 * chunks, chunks)], 3),
+            (stiff_hbm, stiff, 4),
+        ]
     ]
     for copy in copies:
         copy.start()
+    first, last = s == 0, s == n_sub - 1
+    partners = [(dq, ds) for ds in (0, 1, -1) for dq in range(n_mesh) if dq or ds]
     barrier = pltpu.get_barrier_semaphore()
-    partners = [(dq, ds) for ds in (0, -1, 1) for dq in range(n_mesh) if dq or ds]
     for device in partners:
-        pl.semaphore_signal(barrier, inc=1, device_id=at(*device), device_id_type=MESH)
+        if device[1] != 1:
+            pl.semaphore_signal(barrier, inc=1, device_id=at(*device), device_id_type=MESH)
+
+    @pl.when(jnp.logical_not(last))
+    def _():
+        for device in partners:
+            if device[1] == 1:
+                pl.semaphore_signal(barrier, inc=1, device_id=at(*device), device_id_type=MESH)
 
     lane = iota((8, LANES), 1)
     plane = iota((8, LANES), 0)
@@ -161,8 +164,9 @@
         base[pl.ds(8 * p, 8), :] = flat
     base[pl.ds(48, 8), :] = flat - 1.0
 
-    for copy in copies[:9]:
-        copy.wait()
+    landed(inbox.at[pl.ds(0, 152)], 0).wait()
+    copies[2].wait()
+    copies[3].wait()
 
     for a in range(2):
         slowness = TIME_STEP / mass[pl.ds(8 * a, 8), :]
@@ -193,8 +197,7 @@
         for j, (what, i) in enumerate(zip((here, here, speed, point), ids)):
             border[k, pl.ds(8 * j, 8), :] = what[i]
 
-    copies[9].wait()
-    copies[10].wait()
+    landed(raw, 3).wait()
     parts = [raw[pl.ds(chunks * c, chunks), :] for c in range(7)]
     root = jnp.sqrt(parts[6])
     normal = [root * parts[3 + m] for m in range(3)]
@@ -203,47 +206,53 @@
         for h in range(2):
             tables[q, pl.ds(2 * c + h, half, stride=8), :] = values[half * h : half * (h + 1)]
 
-    pl.semaphore_wait(barrier, len(partners))
-
-    edge_copies = {}
-    for i, (dq, ds) in enumerate(NEAR):
-        edge_copies[dq, ds] = pltpu.make_async_remote_copy(
-            src_ref=edge,
-            dst_ref=edges.at[i],
-            send_sem=edge_send.at[i],
-            recv_sem=edge_recv.at[i],
-            device_id=at(-dq, -ds),
+    pl.semaphore_wait(barrier, jnp.where(first, 2 * n_mesh - 1, 3 * n_mesh - 1))
+
+    def send(source, target, device, going, coming):
+        return pltpu.make_async_remote_copy(
+            src_ref=source,
+            dst_ref=target,
+            send_sem=sems.at[going],
+            recv_sem=sems.at[coming],
+            device_id=at(*device),
             device_id_type=MESH,
         )
-    border_copies = [
-        pltpu.make_async_remote_copy(
-            src_ref=border.at[k],
-            dst_ref=borders.at[k],
-            send_sem=border_send.at[k],
-            recv_sem=border_recv.at[k],
-            device_id=at(dq, 0),
-            device_id_type=MESH,
-        )
-        for k, dq in enumerate((1, -1))
-    ]
-    table_copies = {}
-    for i, (dq, ds) in enumerate(partners):
-        table_copies[dq, ds] = pltpu.make_async_remote_copy(
-            src_ref=tables.at[q],
-            dst_ref={0: tables.at[q], 1: distant.at[q], -1: distant.at[n_mesh + q]}[ds],
-            send_sem=table_send.at[i],
-            recv_sem=table_recv.at[i],
-            device_id=at(dq, ds),
-            device_id_type=MESH,
-        )
-    for copy in edge_copies.values():
-        copy.start()
+
+    edge_copies, table_copies = {}, {}
+    for i, (dq, ds) in enumerate(NEAR):
+        edge_copies[-dq, -ds] = send(edge, edges.at[i], (-dq, -ds), 5, 9)
+    border_copies = [send(border.at[k], borders.at[k], (dq, 0), 6, 10) for k, dq in enumerate((1, -1))]
+    for dq, ds in partners:
+        target = {0: tables.at[q], 1: distant.at[q], -1: distant.at[n_mesh + q]}[ds]
+        table_copies[dq, ds] = send(tables.at[q], target, (dq, ds), 7 if ds == 0 else 8, 11 if ds == 0 else 12)
+
+    def start(side):
+        for copies_of in (edge_copies, table_copies):
+            for device, copy in copies_of.items():
+                if device[1] == side:
+                    copy.start()
+
+    @pl.when(last)
+    def _():
+        start(1)
+        for dq in range(n_mesh):
+            pl.semaphore_signal(ready, inc=1, device_id=at(dq, 1), device_id_type=MESH)
+
     for copy in border_copies:
         copy.start()
-    for copy in table_copies.values():
-        copy.start()
-
-    copies[11].wait()
+    start(0)
+
+    @pl.when(jnp.logical_not(last))
+    def _():
+        start(1)
+
+    @pl.when(first)
+    def _():
+        pl.semaphore_wait(ready, n_mesh)
+
+    start(-1)
+
+    landed(stiff, 4).wait()
     weights = coefficients(stiff[...])
 
     def elastic(first, second):
@@ -309,16 +318,13 @@
     force = {}
     for i in (1, 3, 5):
         force[i], force[i + 1] = elastic(around(rows, i), around(rows, i + 1))
-    for copy in border_copies:
-        copy.wait_recv()
+    landed(borders, 10).wait()
     for i, (k, j) in {-2: (0, 0), -1: (0, 1), 8: (1, 0), 9: (1, 1)}.items():
         here[i] = borders[k, pl.ds(8 * j, 8), :]
         rows[i] = turned(here[i])
     force[0], force[7] = elastic(around(rows, 0), around(rows, 7))
     force[-1], force[8] = elastic(around(rows, -1), around(rows, 8))
-    for device, copy in table_copies.items():
-        if device[1] == 0:
-            copy.wait_recv()
+    landed(tables.at[pl.ds(0, n_mesh - 1)], 11).wait()
     later = {}
     after, fast = {}, {}
     for i in range(ROWS):
@@ -332,8 +338,7 @@
         after[i] = ring_step(here[i], moving, push_of(facet, at_point) - force[i])
     shifted = {i: (roll(after[i], 1), roll(after[i], -1)) for i in range(-1, 9)}
 
-    for copy in edge_copies.values():
-        copy.wait_recv()
+    landed(edges, 9).wait()
 
     def column(ds):
         middle = sent if ds == 0 else edges[NEAR.index((0, ds))]
@@ -348,9 +353,7 @@
     )
     strip_speed = [roll(x, -3) for x in strips]
     strip_point = [roll(x, 3) for x in strips]
-    for device, copy in table_copies.items():
-        if device[1] != 0:
-            copy.wait_recv()
+    landed(distant, 12).wait()
     strip_after = []
     for k in range(2):
         outer = place_in == (3, 4)[k]
@@ -381,8 +384,8 @@
         out_vel[pl.ds(i, 6, stride=8), :] = past[0:6]
         out_disp[pl.ds(i, 6, stride=8), :] = (mid + TIME_STEP * past)[0:6]
 
-    for copy in list(edge_copies.values()) + border_copies + list(table_copies.values()):
-        copy.wait_send()
+    for ref, i in ((edges, 5), (border, 6), (tables.at[pl.ds(0, n_mesh - 1)], 7), (distant, 8)):
+        landed(ref, i).wait()
 
 
 def flush(moved, speed, out_moved, out_speed, sem):
@@ -425,10 +428,7 @@
         scratch_shapes=[
             pltpu.VMEM((24, 24), F32),
             pltpu.SMEM((steps, ROWS), jnp.int32),
-            pltpu.VMEM((8 * ROWS, LANES), F32),
-            pltpu.VMEM((8 * ROWS, LANES), F32),
-            pltpu.VMEM((2 * ROWS, LANES), F32),
-            pltpu.VMEM((8 * ROWS, LANES), F32),
+            pltpu.VMEM((24 * ROWS, LANES), F32),
             pltpu.VMEM((8 * ROWS, LANES), F32),
             pltpu.VMEM((steps * ROWS, LANES), jnp.int32),
             pltpu.VMEM((7 * width // LANES, LANES), F32),
@@ -438,13 +438,8 @@
             pltpu.VMEM((2, 32, LANES), F32),
             pltpu.VMEM((8, 8, LANES), F32),
             pltpu.VMEM((2, 32, LANES), F32),
-            dma((12,)),
-            dma((3 * n_mesh - 1,)),
-            dma((3 * n_mesh - 1,)),
-            dma((8,)),
-            dma((8,)),
-            dma((2,)),
-            dma((2,)),
+            dma((13,)),
+            pltpu.SemaphoreType.REGULAR,
         ],
         compiler_params=pltpu.CompilerParams(collective_id=0, has_side_effects=True),
     )(

time: 13 us -> 12 us (0.923)
  the two profiles are of different devices: /device:TPU:0 before, /device:TPU:25 now
where the time goes in v2:
time: 12 us; the launch traced here: 11.8 us
  Pallas kernels  11.1 us (92%)
  between operations  0.64 us (5%)
    pallas_call x1, Pallas kernels, shards(): pl.pallas_call(functools.partial(kernel, n_mesh, n_sub, width), out_shape...  10.5 us
    pallas_call x1, Pallas kernels, shards(): pl.pallas_call(flush, out_shape=[jax.ShapeDtypeStruct((6 * ROWS, LANES),...  0.64 us

profile of v2, /device:TPU:25, one launch (start us, length us, event | category | flops | bytes accessed | tf_op | source)
XLA Modules:
  0.0 11.8 jit_solution(14178887628845403648)
XLA Ops:
  0.6 10.5 %shard_map.113 = (f32[48,128]{1,0:T(8,128)S(1)}, f32[48,128]{1,0:T(8,128)S(1)}) custom-call(f32[24,24]{1,0:T(8,128)} %stiff_hbm.1, s32[2,8]{1,0:T(2,128)} %bitcast.19, f32[48,128]{1,0:T(8,128)} %bitcast.11, f32[48,128]{1,0:T(8,128)} %bitcast.12, f32[16,128]{1,0:T(8,128)} %bitcast.15, f32[16,128]{1,0:T(8,128)} %bitcast.16, f32[24,128]{1,0:T(8,128)} %bitcast.14, ...), custom_call_target="tpu_custom_call" | custom-call | tf_op jit(solution)/shard_map/pallas_call | solution.py:423
  11.1 0.6 %shard_map.114 = (f32[48,128]{1,0:T(8,128)}, f32[48,128]{1,0:T(8,128)}) custom-call(f32[48,128]{1,0:T(8,128)S(1)} %get-tuple-element.6.moved, f32[48,128]{1,0:T(8,128)S(1)} %get-tuple-element.7.speed), custom_call_target="tpu_custom_call" | custom-call | tf_op jit(solution)/shard_map/pallas_call | solution.py:457

commit v3 on v2

--- a/solution.py
+++ b/solution.py
@@ -17,7 +17,6 @@
 BF16 = jnp.bfloat16
 BLOCKS = 9 * 8
 DEPTH = BLOCKS + 8
-NEAR = [(dq, ds) for dq in (-1, 0, 1) for ds in (-1, 0, 1) if dq or ds]
 
 
 def roll(x, shift):
@@ -105,6 +104,8 @@
     border,
     edges,
     borders,
+    note,
+    noted,
     sems,
     ready,
 ):
@@ -118,7 +119,12 @@
     def at(dq, ds):
         return (lax.rem(q + dq + n_mesh, n_mesh), lax.rem(s + ds + n_sub, n_sub))
 
-    def landed(ref, i):
+    size = 4 * chunks
+    planar = 2 * 8 + 2 * 32 + (n_mesh - 1) * size
+    direct = 3 * 8 + n_mesh * size
+
+    def landed(rows, i):
+        ref = distant.at[pl.ds(0, rows)]
         return pltpu.make_async_copy(ref, ref, sems.at[i])
 
     copies = [
@@ -140,18 +146,35 @@
     ]
     for copy in copies:
         copy.start()
-    first, last = s == 0, s == n_sub - 1
-    partners = [(dq, ds) for ds in (0, 1, -1) for dq in range(n_mesh) if dq or ds]
+    first, last, odd = s == 0, s == n_sub - 1, lax.rem(s, 2) == 1
+    from_last, from_above = first, odd & (s != n_sub - 1)
+    to_below = jnp.logical_not(odd | first)
     barrier = pltpu.get_barrier_semaphore()
-    for device in partners:
-        if device[1] != 1:
-            pl.semaphore_signal(barrier, inc=1, device_id=at(*device), device_id_type=MESH)
-
-    @pl.when(jnp.logical_not(last))
-    def _():
-        for device in partners:
-            if device[1] == 1:
-                pl.semaphore_signal(barrier, inc=1, device_id=at(*device), device_id_type=MESH)
+
+    def hello(dq, ds):
+        pl.semaphore_signal(barrier, inc=1, device_id=at(dq, ds), device_id_type=MESH)
+
+    for dq in range(1, n_mesh):
+        hello(dq, 0)
+
+    @pl.when(first)
+    def _():
+        hello(0, 1)
+        for dq in range(n_mesh):
+            hello(dq, -1)
+
+    @pl.when(jnp.logical_not(first))
+    def _():
+        hello(0, -1)
+
+    @pl.when(from_above)
+    def _():
+        for dq in range(n_mesh):
+            hello(dq, 1)
+
+    @pl.when(to_below)
+    def _():
+        hello(0, 1)
 
     lane = iota((8, LANES), 1)
     plane = iota((8, LANES), 0)
@@ -164,7 +187,7 @@
         base[pl.ds(8 * p, 8), :] = flat
     base[pl.ds(48, 8), :] = flat - 1.0
 
-    landed(inbox.at[pl.ds(0, 152)], 0).wait()
+    landed(152, 0).wait()
     copies[2].wait()
     copies[3].wait()
 
@@ -197,7 +220,7 @@
         for j, (what, i) in enumerate(zip((here, here, speed, point), ids)):
             border[k, pl.ds(8 * j, 8), :] = what[i]
 
-    landed(raw, 3).wait()
+    landed(7 * chunks, 3).wait()
     parts = [raw[pl.ds(chunks * c, chunks), :] for c in range(7)]
     root = jnp.sqrt(parts[6])
     normal = [root * parts[3 + m] for m in range(3)]
@@ -206,7 +229,8 @@
         for h in range(2):
             tables[q, pl.ds(2 * c + h, half, stride=8), :] = values[half * h : half * (h + 1)]
 
-    pl.semaphore_wait(barrier, jnp.where(first, 2 * n_mesh - 1, 3 * n_mesh - 1))
+    expected = n_mesh - 1 + jnp.where(first, 1, jnp.where(odd, jnp.where(last, n_mesh + 1, 2), n_mesh + 1))
+    pl.semaphore_wait(barrier, expected)
 
     def send(source, target, device, going, coming):
         return pltpu.make_async_remote_copy(
@@ -214,45 +238,39 @@
             dst_ref=target,
             send_sem=sems.at[going],
             recv_sem=sems.at[coming],
-            device_id=at(*device),
+            device_id=device,
             device_id_type=MESH,
         )
 
-    edge_copies, table_copies = {}, {}
-    for i, (dq, ds) in enumerate(NEAR):
-        edge_copies[-dq, -ds] = send(edge, edges.at[i], (-dq, -ds), 5, 9)
-    border_copies = [send(border.at[k], borders.at[k], (dq, 0), 6, 10) for k, dq in enumerate((1, -1))]
-    for dq, ds in partners:
-        target = {0: tables.at[q], 1: distant.at[q], -1: distant.at[n_mesh + q]}[ds]
-        table_copies[dq, ds] = send(tables.at[q], target, (dq, ds), 7 if ds == 0 else 8, 11 if ds == 0 else 12)
-
-    def start(side):
-        for copies_of in (edge_copies, table_copies):
-            for device, copy in copies_of.items():
-                if device[1] == side:
-                    copy.start()
+    def send_direct(ds):
+        for dq in (0, 1, -1):
+            send(edge, edges.at[2 - dq], at(dq, ds), 6, 13).start()
+        for t in range(n_mesh):
+            device = (t, lax.rem(s + ds + n_sub, n_sub))
+            send(tables.at[q], distant.at[pl.ds(pl.multiple_of(q * size, size), size)], device, 6, 14).start()
 
     @pl.when(last)
     def _():
-        start(1)
-        for dq in range(n_mesh):
-            pl.semaphore_signal(ready, inc=1, device_id=at(dq, 1), device_id_type=MESH)
-
-    for copy in border_copies:
-        copy.start()
-    start(0)
-
-    @pl.when(jnp.logical_not(last))
-    def _():
-        start(1)
-
-    @pl.when(first)
-    def _():
-        pl.semaphore_wait(ready, n_mesh)
-
-    start(-1)
-
-    landed(stiff, 4).wait()
+        send_direct(1)
+        pl.semaphore_signal(ready, inc=1, device_id=at(0, 1), device_id_type=MESH)
+
+    for t in range(n_mesh):
+        for k, dq in enumerate((1, -1)):
+
+            @pl.when(lax.rem(q + dq + n_mesh, n_mesh) == t)
+            def _():
+                send(border.at[k], borders.at[k], (t, s), 5, 9).start()
+                send(edge, edges.at[4 * k], (t, s), 5, 9).start()
+
+        @pl.when(q != t)
+        def _():
+            send(tables.at[q], tables.at[q], (t, s), 5, 10).start()
+
+    @pl.when(to_below)
+    def _():
+        send_direct(-1)
+
+    copies[11].wait()
     weights = coefficients(stiff[...])
 
     def elastic(first, second):
@@ -283,23 +301,24 @@
             total = jnp.where(chunk == k, picked, total)
         return narrowed(total, second)
 
-    def facet_by(code, sides, choice):
-        code = code.astype(jnp.int32)
+    def facet_by(at_point, ref):
+        code = jnp.broadcast_to(at_point[7:8], (8, LANES)).astype(jnp.int32)
         owner, index = code >> bits, code & (width - 1)
         chunk, place = index >> 7, index & (LANES - 1)
         second = chunk >= half
         chunk = jnp.where(second, chunk - half, chunk) + half * owner
-        if choice is not None:
-            chunk = chunk + choice * (half * n_mesh)
         total = flat
-        for side in sides:
-            for o in range(n_mesh):
-                for k in range(half):
-                    ref, at_slot = (distant, (side - 1) * n_mesh + o) if side else (tables, o)
-                    rows = ref[at_slot, pl.ds(8 * k, 8), :]
-                    picked = jnp.take_along_axis(rows, place, axis=1, mode="promise_in_bounds")
-                    total = jnp.where(chunk == (side * n_mesh + o) * half + k, picked, total)
+        for k in range(half * n_mesh):
+            rows = ref(k)
+            picked = jnp.take_along_axis(rows, place, axis=1, mode="promise_in_bounds")
+            total = jnp.where(chunk == k, picked, total)
         return narrowed(total, second)
+
+    def of_plane(k):
+        return tables[k // half, pl.ds(8 * (k % half), 8), :]
+
+    def of_side(k):
+        return distant[pl.ds(8 * k, 8), :]
 
     def push_of(facet, at_point):
         product = jnp.where(surface | (plane == 6), facet * at_point, 0.0)
@@ -318,13 +337,37 @@
     force = {}
     for i in (1, 3, 5):
         force[i], force[i + 1] = elastic(around(rows, i), around(rows, i + 1))
-    landed(borders, 10).wait()
+    landed(2 * 8 + 2 * 32, 9).wait()
     for i, (k, j) in {-2: (0, 0), -1: (0, 1), 8: (1, 0), 9: (1, 1)}.items():
         here[i] = borders[k, pl.ds(8 * j, 8), :]
         rows[i] = turned(here[i])
     force[0], force[7] = elastic(around(rows, 0), around(rows, 7))
     force[-1], force[8] = elastic(around(rows, -1), around(rows, 8))
-    landed(tables.at[pl.ds(0, n_mesh - 1)], 11).wait()
+
+    def column(middle, before, behind):
+        return jnp.where(group < 8, middle, jnp.where(group < 12, behind, before))
+
+    centre = column(sent, edges[0], edges[4])
+    landed((n_mesh - 1) * size, 10).wait()
+    own_point = roll(centre, 3)
+    own_push = push_of(facet_by(own_point, of_plane), own_point)
+
+    note[0] = centre
+    note[1] = own_push
+
+    @pl.when(jnp.logical_not(last))
+    def _():
+        send(note, noted.at[0], at(0, 1), 7, 11).start()
+
+    @pl.when(odd)
+    def _():
+        send(note, noted.at[1], at(0, -1), 8, 12).start()
+
+    @pl.when(first)
+    def _():
+        pl.semaphore_wait(ready, 1)
+        send(note, noted.at[1], at(0, -1), 8, 12).start()
+
     later = {}
     after, fast = {}, {}
     for i in range(ROWS):
@@ -334,34 +377,44 @@
         after[i] = jnp.where(entry, here[i] + TIME_STEP * fast[i], here[i])
     for i, k in ((-1, 0), (8, 1)):
         moving, at_point = borders[k, pl.ds(16, 8), :], borders[k, pl.ds(24, 8), :]
-        facet = facet_by(jnp.broadcast_to(at_point[7:8], (8, LANES)), (0,), None)
+        facet = facet_by(at_point, of_plane)
         after[i] = ring_step(here[i], moving, push_of(facet, at_point) - force[i])
     shifted = {i: (roll(after[i], 1), roll(after[i], -1)) for i in range(-1, 9)}
 
-    landed(edges, 9).wait()
-
-    def column(ds):
-        middle = sent if ds == 0 else edges[NEAR.index((0, ds))]
-        beyond = jnp.where(group < 12, edges[NEAR.index((1, ds))], edges[NEAR.index((-1, ds))])
-        return jnp.where(group < 8, middle, beyond)
-
-    left, centre, right = column(-1), column(0), column(1)
+    has_direct = from_last | from_above
+
+    @pl.when(jnp.logical_not(from_above))
+    def _():
+        landed(2 * 8, 12).wait()
+
+    @pl.when(jnp.logical_not(first))
+    def _():
+        landed(2 * 8, 11).wait()
+
+    @pl.when(has_direct)
+    def _():
+        landed(3 * 8, 13).wait()
+
+    far = column(edges[2], edges[1], edges[3])
+    left, right = jnp.where(from_last, far, noted[0, 0]), jnp.where(from_above, far, noted[1, 0])
     from_before = (place_in == 0) | (place_in == 2) | (place_in == 3) | (place_in == 6)
     strips = [jnp.where(from_before, left, centre), jnp.where(from_before, centre, right)]
     strip_force = elastic(
         *([roll(x, -(GROUP * di + dj)) for di in (-1, 0, 1) for dj in (-1, 0, 1)] for x in strips)
     )
     strip_speed = [roll(x, -3) for x in strips]
-    strip_point = [roll(x, 3) for x in strips]
-    landed(distant, 12).wait()
+    far_point = roll(far, 3)
+
+    @pl.when(has_direct)
+    def _():
+        landed(n_mesh * size, 14).wait()
+
+    far_push = push_of(facet_by(far_point, of_side), far_point)
     strip_after = []
-    for k in range(2):
-        outer = place_in == (3, 4)[k]
-        facet = facet_by(
-            jnp.broadcast_to(strip_point[k][7:8], (8, LANES)), (0, 1 + k), jnp.where(outer, 1 + k, 0)
-        )
-        net = push_of(facet, strip_point[k]) - strip_force[k]
-        strip_after.append(ring_step(strips[k], strip_speed[k], net))
+    for k, by_far in enumerate((from_last, from_above)):
+        push = jnp.where(by_far, far_push, noted[k, 1])
+        push = jnp.where(place_in == (3, 4)[k], push, own_push)
+        strip_after.append(ring_step(strips[k], strip_speed[k], push - strip_force[k]))
     corner = jnp.where(place_in == 4, strip_after[0], strip_after[1])
 
     rows = {}
@@ -384,8 +437,19 @@
         out_vel[pl.ds(i, 6, stride=8), :] = past[0:6]
         out_disp[pl.ds(i, 6, stride=8), :] = (mid + TIME_STEP * past)[0:6]
 
-    for ref, i in ((edges, 5), (border, 6), (tables.at[pl.ds(0, n_mesh - 1)], 7), (distant, 8)):
-        landed(ref, i).wait()
+    landed(planar, 5).wait()
+
+    @pl.when(to_below | last)
+    def _():
+        landed(direct, 6).wait()
+
+    @pl.when(jnp.logical_not(last))
+    def _():
+        landed(2 * 8, 7).wait()
+
+    @pl.when(odd | first)
+    def _():
+        landed(2 * 8, 8).wait()
 
 
 def flush(moved, speed, out_moved, out_speed, sem):
@@ -414,7 +478,7 @@
     steps = owners.shape[0]
     width = facets.shape[3]
     n_mesh, n_sub = lax.axis_size("mesh"), lax.axis_size("sub")
-    assert displacement.shape == (3, 2, ROWS, LANES) and steps == 2
+    assert displacement.shape == (3, 2, ROWS, LANES) and steps == 2 and n_sub % 2 == 0
     assert width == 1 << (width.bit_length() - 1) and width >= 2 * LANES
     out = pltpu.VMEM((6 * ROWS, LANES), F32)
     anywhere = pl.BlockSpec(memory_space=pl.ANY)
@@ -433,12 +497,14 @@
             pltpu.VMEM((steps * ROWS, LANES), jnp.int32),
             pltpu.VMEM((7 * width // LANES, LANES), F32),
             pltpu.VMEM((n_mesh, 4 * width // LANES, LANES), F32),
-            pltpu.VMEM((2 * n_mesh, 4 * width // LANES, LANES), F32),
+            pltpu.VMEM((n_mesh * 4 * width // LANES + 128, LANES), F32),
             pltpu.VMEM((8, LANES), F32),
             pltpu.VMEM((2, 32, LANES), F32),
-            pltpu.VMEM((8, 8, LANES), F32),
+            pltpu.VMEM((5, 8, LANES), F32),
             pltpu.VMEM((2, 32, LANES), F32),
-            dma((13,)),
+            pltpu.VMEM((2, 8, LANES), F32),
+            pltpu.VMEM((2, 2, 8, LANES), F32),
+            dma((15,)),
             pltpu.SemaphoreType.REGULAR,
         ],
         compiler_params=pltpu.CompilerParams(collective_id=0, has_side_effects=True),

time: 12 us -> 11.1 us (0.925)
  the two profiles are of different devices: /device:TPU:25 before, /device:TPU:0 now
where the time goes in v3:
time: 11.1 us; the launch traced here: 10.9 us
  Pallas kernels  10.2 us (92%)
  between operations  0.64 us (6%)
    pallas_call x1, Pallas kernels, shards(): pl.pallas_call(functools.partial(kernel, n_mesh, n_sub, width), out_shape...  9.6 us
    pallas_call x1, Pallas kernels, shards(): pl.pallas_call(flush, out_shape=[jax.ShapeDtypeStruct((6 * ROWS, LANES),...  0.64 us

profile of v3, /device:TPU:0, one launch (start us, length us, event | category | flops | bytes accessed | tf_op | source)
XLA Modules:
  0.0 10.9 jit_solution(3640855750429119985)
XLA Ops:
  0.6 9.6 %shard_map.113 = (f32[48,128]{1,0:T(8,128)S(1)}, f32[48,128]{1,0:T(8,128)S(1)}) custom-call(f32[24,24]{1,0:T(8,128)} %stiff_hbm.1, s32[2,8]{1,0:T(2,128)} %bitcast.19, f32[48,128]{1,0:T(8,128)} %bitcast.11, f32[48,128]{1,0:T(8,128)} %bitcast.12, f32[16,128]{1,0:T(8,128)} %bitcast.15, f32[16,128]{1,0:T(8,128)} %bitcast.16, f32[24,128]{1,0:T(8,128)} %bitcast.14, ...), custom_call_target="tpu_custom_call" | custom-call | tf_op jit(solution)/shard_map/pallas_call | solution.py:487
  10.2 0.6 %shard_map.114 = (f32[48,128]{1,0:T(8,128)}, f32[48,128]{1,0:T(8,128)}) custom-call(f32[48,128]{1,0:T(8,128)S(1)} %get-tuple-element.6.moved, f32[48,128]{1,0:T(8,128)S(1)} %get-tuple-element.7.speed), custom_call_target="tpu_custom_call" | custom-call | tf_op jit(solution)/shard_map/pallas_call | solution.py:523

commit v4 on v3

--- a/solution.py
+++ b/solution.py
@@ -132,16 +132,16 @@
         for src, dst, i in [
             (disp_hbm, own.at[pl.ds(0, 48)], 0),
             (moduli_hbm, own.at[pl.ds(48, 16)], 0),
-            (owners_hbm, owners, 2),
-            (pairs_hbm, pairs, 1),
+            (owners_hbm, owners, 1),
+            (pairs_hbm, pairs, 0),
             (vel_hbm, vel.at[pl.ds(0, 48)], 0),
             (mass_hbm, mass, 0),
         ]
         + [(surf_hbm.at[pl.ds(8 * m, 8)], base.at[pl.ds(16 * m, 8)], 0) for m in range(3)]
         + [
-            (facets_hbm, raw.at[pl.ds(0, 6 * chunks)], 3),
-            (penalty_hbm, raw.at[pl.ds(6 * chunks, chunks)], 3),
-            (stiff_hbm, stiff, 4),
+            (facets_hbm, raw.at[pl.ds(0, 6 * chunks)], 2),
+            (penalty_hbm, raw.at[pl.ds(6 * chunks, chunks)], 2),
+            (stiff_hbm, stiff, 3),
         ]
     ]
     for copy in copies:
@@ -187,9 +187,8 @@
         base[pl.ds(8 * p, 8), :] = flat
     base[pl.ds(48, 8), :] = flat - 1.0
 
-    landed(152, 0).wait()
+    landed(152 + 16, 0).wait()
     copies[2].wait()
-    copies[3].wait()
 
     for a in range(2):
         slowness = TIME_STEP / mass[pl.ds(8 * a, 8), :]
@@ -220,7 +219,7 @@
         for j, (what, i) in enumerate(zip((here, here, speed, point), ids)):
             border[k, pl.ds(8 * j, 8), :] = what[i]
 
-    landed(7 * chunks, 3).wait()
+    landed(7 * chunks, 2).wait()
     parts = [raw[pl.ds(chunks * c, chunks), :] for c in range(7)]
     root = jnp.sqrt(parts[6])
     normal = [root * parts[3 + m] for m in range(3)]
@@ -243,11 +242,30 @@
         )
 
     def send_direct(ds):
+        place = pl.multiple_of(q * size, size)
+
+        def to(t):
+            device = (t, lax.rem(s + ds + n_sub, n_sub))
+            send(tables.at[q], distant.at[pl.ds(place, size)], device, 1, 8).start()
+
+        def edge_to(dq):
+            send(edge, edges.at[2 - dq], at(dq, ds), 1, 7).start()
+
         for dq in (0, 1, -1):
-            send(edge, edges.at[2 - dq], at(dq, ds), 6, 13).start()
-        for t in range(n_mesh):
-            device = (t, lax.rem(s + ds + n_sub, n_sub))
-            send(tables.at[q], distant.at[pl.ds(pl.multiple_of(q * size, size), size)], device, 6, 14).start()
+
+            @pl.when(at(dq, 0)[0] == 0)
+            def _():
+                edge_to(dq)
+
+        to(0)
+        for dq in (0, 1, -1):
+
+            @pl.when(at(dq, 0)[0] != 0)
+            def _():
+                edge_to(dq)
+
+        for t in range(1, n_mesh):
+            to(t)
 
     @pl.when(last)
     def _():
@@ -259,12 +277,12 @@
 
             @pl.when(lax.rem(q + dq + n_mesh, n_mesh) == t)
             def _():
-                send(border.at[k], borders.at[k], (t, s), 5, 9).start()
-                send(edge, edges.at[4 * k], (t, s), 5, 9).start()
+                send(border.at[k], borders.at[k], (t, s), 0, 4).start()
+                send(edge, edges.at[4 * k], (t, s), 0, 4).start()
 
         @pl.when(q != t)
         def _():
-            send(tables.at[q], tables.at[q], (t, s), 5, 10).start()
+            send(tables.at[q], tables.at[q], (t, s), 0, 5).start()
 
     @pl.when(to_below)
     def _():
@@ -337,7 +355,7 @@
     force = {}
     for i in (1, 3, 5):
         force[i], force[i + 1] = elastic(around(rows, i), around(rows, i + 1))
-    landed(2 * 8 + 2 * 32, 9).wait()
+    landed(2 * 8 + 2 * 32, 4).wait()
     for i, (k, j) in {-2: (0, 0), -1: (0, 1), 8: (1, 0), 9: (1, 1)}.items():
         here[i] = borders[k, pl.ds(8 * j, 8), :]
         rows[i] = turned(here[i])
@@ -348,7 +366,7 @@
         return jnp.where(group < 8, middle, jnp.where(group < 12, behind, before))
 
     centre = column(sent, edges[0], edges[4])
-    landed((n_mesh - 1) * size, 10).wait()
+    landed((n_mesh - 1) * size, 5).wait()
     own_point = roll(centre, 3)
     own_push = push_of(facet_by(own_point, of_plane), own_point)
 
@@ -357,16 +375,16 @@
 
     @pl.when(jnp.logical_not(last))
     def _():
-        send(note, noted.at[0], at(0, 1), 7, 11).start()
+        send(note, noted.at[0], at(0, 1), 2, 6).start()
 
     @pl.when(odd)
     def _():
-        send(note, noted.at[1], at(0, -1), 8, 12).start()
+        send(note, noted.at[1], at(0, -1), 3, 6).start()
 
     @pl.when(first)
     def _():
         pl.semaphore_wait(ready, 1)
-        send(note, noted.at[1], at(0, -1), 8, 12).start()
+        send(note, noted.at[1], at(0, -1), 3, 6).start()
 
     later = {}
     after, fast = {}, {}
@@ -383,17 +401,14 @@
 
     has_direct = from_last | from_above
 
-    @pl.when(jnp.logical_not(from_above))
-    def _():
-        landed(2 * 8, 12).wait()
-
-    @pl.when(jnp.logical_not(first))
-    def _():
-        landed(2 * 8, 11).wait()
+    @pl.when(jnp.logical_not(has_direct))
+    def _():
+        landed(2 * 2 * 8, 6).wait()
 
     @pl.when(has_direct)
     def _():
-        landed(3 * 8, 13).wait()
+        landed(2 * 8, 6).wait()
+        landed(3 * 8, 7).wait()
 
     far = column(edges[2], edges[1], edges[3])
     left, right = jnp.where(from_last, far, noted[0, 0]), jnp.where(from_above, far, noted[1, 0])
@@ -407,7 +422,7 @@
 
     @pl.when(has_direct)
     def _():
-        landed(n_mesh * size, 14).wait()
+        landed(n_mesh * size, 8).wait()
 
     far_push = push_of(facet_by(far_point, of_side), far_point)
     strip_after = []
@@ -437,19 +452,19 @@
         out_vel[pl.ds(i, 6, stride=8), :] = past[0:6]
         out_disp[pl.ds(i, 6, stride=8), :] = (mid + TIME_STEP * past)[0:6]
 
-    landed(planar, 5).wait()
+    landed(planar, 0).wait()
 
     @pl.when(to_below | last)
     def _():
-        landed(direct, 6).wait()
+        landed(direct, 1).wait()
 
     @pl.when(jnp.logical_not(last))
     def _():
-        landed(2 * 8, 7).wait()
+        landed(2 * 8, 2).wait()
 
     @pl.when(odd | first)
     def _():
-        landed(2 * 8, 8).wait()
+        landed(2 * 8, 3).wait()
 
 
 def flush(moved, speed, out_moved, out_speed, sem):
@@ -504,7 +519,7 @@
             pltpu.VMEM((2, 32, LANES), F32),
             pltpu.VMEM((2, 8, LANES), F32),
             pltpu.VMEM((2, 2, 8, LANES), F32),
-            dma((15,)),
+            dma((9,)),
             pltpu.SemaphoreType.REGULAR,
         ],
         compiler_params=pltpu.CompilerParams(collective_id=0, has_side_effects=True),

time: 11.1 us -> 11 us (level)
  no operation moved by 1% of the time
where the time goes in v4:
time: 11 us; the launch traced here: 10.8 us
  Pallas kernels  10.2 us (93%)
  between operations  0.64 us (6%)
    pallas_call x1, Pallas kernels, shards(): pl.pallas_call(functools.partial(kernel, n_mesh, n_sub, width), out_shape...  9.51 us
    pallas_call x1, Pallas kernels, shards(): pl.pallas_call(flush, out_shape=[jax.ShapeDtypeStruct((6 * ROWS, LANES),...  0.64 us

profile of v4, /device:TPU:0, one launch (start us, length us, event | category | flops | bytes accessed | tf_op | source)
XLA Modules:
  0.0 10.8 jit_solution(17945749656525309802)
XLA Ops:
  0.6 9.5 %shard_map.113 = (f32[48,128]{1,0:T(8,128)S(1)}, f32[48,128]{1,0:T(8,128)S(1)}) custom-call(f32[24,24]{1,0:T(8,128)} %stiff_hbm.1, s32[2,8]{1,0:T(2,128)} %bitcast.19, f32[48,128]{1,0:T(8,128)} %bitcast.11, f32[48,128]{1,0:T(8,128)} %bitcast.12, f32[16,128]{1,0:T(8,128)} %bitcast.15, f32[16,128]{1,0:T(8,128)} %bitcast.16, f32[24,128]{1,0:T(8,128)} %bitcast.14, ...), custom_call_target="tpu_custom_call" | custom-call | tf_op jit(solution)/shard_map/pallas_call | solution.py:502
  10.2 0.6 %shard_map.114 = (f32[48,128]{1,0:T(8,128)}, f32[48,128]{1,0:T(8,128)}) custom-call(f32[48,128]{1,0:T(8,128)S(1)} %get-tuple-element.6.moved, f32[48,128]{1,0:T(8,128)S(1)} %get-tuple-element.7.speed), custom_call_target="tpu_custom_call" | custom-call | tf_op jit(solution)/shard_map/pallas_call | solution.py:538

commit v5 on v4

--- a/solution.py
+++ b/solution.py
@@ -63,10 +63,27 @@
         term = jnp.dot(high, one_hot(place & (third < 2)), preferred_element_type=F32)
         term = term + jnp.dot(low, one_hot(place & (third == 2)), preferred_element_type=F32)
         force = term if force is None else jnp.where((iota((32, 256), 0) >> 3) == group, term, force)
+    third, di, dj, p, used = columns((24, LANES))
+    single = None
+    for group in range(4):
+        b2, e2 = di + (group >> 1), dj + (group & 1)
+        wanted = 3 * (4 * (p & 1) + 2 * b2 + e2) + (p >> 1)
+        place = used & inside(b2, e2) & (p < 6) & (wanted == iota((24, LANES), 0)) & (third == 0)
+        term = jnp.dot(high, one_hot(place), preferred_element_type=F32)
+        term = term + jnp.dot(low, one_hot(place), preferred_element_type=F32)
+        single = term if single is None else jnp.where((iota((32, LANES), 0) >> 3) == group, term, single)
     third, di, dj, p, used = columns((32, 256))
     row = iota((32, 256), 0)
     counted = used & inside(di + (row >> 4), dj + ((row >> 3) & 1)) & (p >= 6) & (third < 2)
-    return jnp.concatenate([force, jnp.where(counted, 0.125, 0.0)], axis=0).astype(BF16)
+    return jnp.concatenate([force, jnp.where(counted, 0.125, 0.0)], axis=0).astype(BF16), single
+
+
+TOUCHED = [
+    [2 * b + e for b in (0, 1) for e in (0, 1) if 0 <= di + b <= 1 and 0 <= dj + e <= 1]
+    for di in (-1, 0, 1)
+    for dj in (-1, 0, 1)
+]
+SPREAD = [(off, p, g) for off in range(9) for p in range(6) for g in TOUCHED[off]]
 
 
 def stacked(blocks):
@@ -106,6 +123,8 @@
     borders,
     note,
     noted,
+    spread,
+    turns,
     sems,
     ready,
 ):
@@ -190,10 +209,6 @@
     landed(152 + 16, 0).wait()
     copies[2].wait()
 
-    for a in range(2):
-        slowness = TIME_STEP / mass[pl.ds(8 * a, 8), :]
-        for p in range(a, 8, 2):
-            inverse[pl.ds(8 * p, 8), :] = slowness
     holder = jnp.zeros((8, LANES), jnp.int32)
     for b in range(ROWS):
         holder = jnp.where(plane == b, owners[0, b], holder)
@@ -203,8 +218,7 @@
         return ref[pl.ds(i, 8, stride=8), :]
 
     here = {i: of_row(own, i) for i in range(ROWS)}
-    gain = {i: of_row(inverse, i) for i in range(ROWS)}
-    speed = {i: jnp.where(entry, of_row(vel, i), gain[i]) for i in range(ROWS)}
+    speed = {i: of_row(vel, i) for i in range(ROWS)}
     point = {i: of_row(base, i) for i in range(ROWS)}
     point = {i: jnp.where(surface, point[i] + here[i], point[i]) for i in range(ROWS)}
 
@@ -288,8 +302,16 @@
     def _():
         send_direct(-1)
 
+    for a in range(2):
+        slowness = TIME_STEP / mass[pl.ds(8 * a, 8), :]
+        for p in range(a, 8, 2):
+            inverse[pl.ds(8 * p, 8), :] = slowness
+    gain = {i: of_row(inverse, i) for i in range(ROWS)}
     copies[11].wait()
-    weights = coefficients(stiff[...])
+    weights, single = coefficients(stiff[...])
+    for n, (off, p, g) in enumerate(SPREAD):
+        column_of = single[8 * g : 8 * g + 8, 8 * off + p : 8 * off + p + 1]
+        spread[pl.ds(8 * n, 8), :] = jnp.broadcast_to(column_of, (8, LANES))
 
     def elastic(first, second):
         blocks = [jnp.concatenate([a, b], axis=1) for a, b in zip(first, second)]
@@ -297,6 +319,33 @@
         terms = [got[8 * g : 8 * g + 8] * got[32 + 8 * g : 40 + 8 * g] for g in range(4)]
         force = (terms[0] + terms[1]) + (terms[2] + terms[3])
         return force[:, :LANES], force[:, LANES:]
+
+    def side_forces(moved):
+        for k, blocks in enumerate(moved):
+            for off, x in enumerate(blocks):
+                turns[pl.ds(72 * k + 8 * off, 8), :] = x
+
+        def plane_of(k, off, p):
+            return jnp.broadcast_to(turns[pl.ds(72 * k + 8 * off + p, 1), :], (8, LANES))
+
+        def plus(table, key, term):
+            table[key] = table[key] + term if key in table else term
+
+        sums, scales, n = {}, {}, 0
+        for off in range(9):
+            for k in range(len(moved)):
+                both = plane_of(k, off, 6) + plane_of(k, off, 7)
+                for g in TOUCHED[off]:
+                    plus(scales, (k, g), both)
+            for p in range(6):
+                values = [plane_of(k, off, p) for k in range(len(moved))]
+                for g in TOUCHED[off]:
+                    factor = spread[pl.ds(8 * n, 8), :]
+                    n += 1
+                    for k, value in enumerate(values):
+                        plus(sums, (k, g), factor * value)
+        terms = {key: sums[key] * (0.125 * scales[key]) for key in sums}
+        return [(terms[k, 0] + terms[k, 1]) + (terms[k, 2] + terms[k, 3]) for k in range(len(moved))]
 
     def around(rows, i):
         return [x for di in (-1, 0, 1) for x in rows[i + di]]
@@ -319,12 +368,15 @@
             total = jnp.where(chunk == k, picked, total)
         return narrowed(total, second)
 
-    def facet_by(at_point, ref):
+    def wanted_by(at_point):
         code = jnp.broadcast_to(at_point[7:8], (8, LANES)).astype(jnp.int32)
         owner, index = code >> bits, code & (width - 1)
         chunk, place = index >> 7, index & (LANES - 1)
         second = chunk >= half
-        chunk = jnp.where(second, chunk - half, chunk) + half * owner
+        return jnp.where(second, chunk - half, chunk) + half * owner, place, second
+
+    def facet_by(wanted, ref):
+        chunk, place, second = wanted
         total = flat
         for k in range(half * n_mesh):
             rows = ref(k)
@@ -345,11 +397,12 @@
         return jnp.where(surface, facet * jnp.maximum(-product, 0.0), 0.0)
 
     def ring_step(values, moving, net):
-        slow = jnp.where(
+        weight = jnp.where(
             (plane & 1) == 0, jnp.broadcast_to(moving[6:7], (8, LANES)), jnp.broadcast_to(moving[7:8], (8, LANES))
         )
+        slow = TIME_STEP / weight
         faster = moving + slow * net
-        return jnp.where(entry, values + TIME_STEP * faster, values)
+        return jnp.where(entry, values + TIME_STEP * faster, values), faster
 
     rows = {i: turned(here[i]) for i in range(ROWS)}
     force = {}
@@ -368,7 +421,7 @@
     centre = column(sent, edges[0], edges[4])
     landed((n_mesh - 1) * size, 5).wait()
     own_point = roll(centre, 3)
-    own_push = push_of(facet_by(own_point, of_plane), own_point)
+    own_push = push_of(facet_by(wanted_by(own_point), of_plane), own_point)
 
     note[0] = centre
     note[1] = own_push
@@ -395,9 +448,32 @@
         after[i] = jnp.where(entry, here[i] + TIME_STEP * fast[i], here[i])
     for i, k in ((-1, 0), (8, 1)):
         moving, at_point = borders[k, pl.ds(16, 8), :], borders[k, pl.ds(24, 8), :]
-        facet = facet_by(at_point, of_plane)
-        after[i] = ring_step(here[i], moving, push_of(facet, at_point) - force[i])
-    shifted = {i: (roll(after[i], 1), roll(after[i], -1)) for i in range(-1, 9)}
+        facet = facet_by(wanted_by(at_point), of_plane)
+        after[i], _ = ring_step(here[i], moving, push_of(facet, at_point) - force[i])
+
+    rows = {i: turned(after[i]) for i in range(-1, 9)}
+    for i in range(0, ROWS, 2):
+        force[i], force[i + 1] = elastic(around(rows, i), around(rows, i + 1))
+    for i in range(ROWS):
+        at_point = of_row(base, i)
+        at_point = jnp.where(surface, at_point + after[i], at_point)
+        past = fast[i] + gain[i] * (push_of(later[i], at_point) - force[i])
+        out_vel[pl.ds(i, 6, stride=8), :] = past[0:6]
+        out_disp[pl.ds(i, 6, stride=8), :] = (after[i] + TIME_STEP * past)[0:6]
+
+    def strip_of(rows_of, indices):
+        made = flat
+        for i in indices:
+            g = i % GROUPS
+            piece = jnp.where(place_in < 4, roll(rows_of[i], GROUP * g + 3), roll(rows_of[i], GROUP * g + 5))
+            made = jnp.where(group == g, piece, made)
+        return made
+
+    known = strip_of(after, range(-1, 9))
+    known_fast, known_gain, known_facet = (strip_of(x, range(ROWS)) for x in (fast, gain, later))
+    known_point = strip_of({i: of_row(base, i) for i in range(ROWS)}, range(ROWS))
+    shifts = (1, -1)
+    own_pushes = [roll(own_push, shift) for shift in shifts]
 
     has_direct = from_last | from_above
 
@@ -414,43 +490,40 @@
     left, right = jnp.where(from_last, far, noted[0, 0]), jnp.where(from_above, far, noted[1, 0])
     from_before = (place_in == 0) | (place_in == 2) | (place_in == 3) | (place_in == 6)
     strips = [jnp.where(from_before, left, centre), jnp.where(from_before, centre, right)]
-    strip_force = elastic(
-        *([roll(x, -(GROUP * di + dj)) for di in (-1, 0, 1) for dj in (-1, 0, 1)] for x in strips)
-    )
-    strip_speed = [roll(x, -3) for x in strips]
-    far_point = roll(far, 3)
+    moved = [
+        [roll(x, shift - (GROUP * di + dj)) for di in (-1, 0, 1) for dj in (-1, 0, 1)]
+        for x, shift in zip(strips, shifts)
+    ]
+    strip_force = side_forces(moved)
+    strip_speed = [roll(x, shift - 3) for x, shift in zip(strips, shifts)]
+    far_point = jnp.where(from_last, roll(far, 3 + shifts[0]), roll(far, 3 + shifts[1]))
+    far_wanted = wanted_by(far_point)
+    noted_push = [roll(noted[k, 1], shifts[k]) for k in range(2)]
 
     @pl.when(has_direct)
     def _():
         landed(n_mesh * size, 8).wait()
 
-    far_push = push_of(facet_by(far_point, of_side), far_point)
+    far_push = push_of(facet_by(far_wanted, of_side), far_point)
     strip_after = []
     for k, by_far in enumerate((from_last, from_above)):
-        push = jnp.where(by_far, far_push, noted[k, 1])
-        push = jnp.where(place_in == (3, 4)[k], push, own_push)
-        strip_after.append(ring_step(strips[k], strip_speed[k], push - strip_force[k]))
-    corner = jnp.where(place_in == 4, strip_after[0], strip_after[1])
-
-    rows = {}
-    for i in range(-1, 9):
-        start = GROUP * (i % GROUPS) + 3
-        mid = jnp.where((lane == 0) | (lane == LANES - 1), roll(corner, -(start + 1)), after[i])
-        before = jnp.where(lane < 2, roll(strip_after[0], -start), shifted[i][0])
-        behind = jnp.where(lane >= LANES - 2, roll(strip_after[1], LANES - 2 - start), shifted[i][1])
-        rows[i] = (before, mid, behind)
-    for i in range(0, ROWS, 2):
-        force[i], force[i + 1] = elastic(around(rows, i), around(rows, i + 1))
-    side = (lane == 0) | (lane == LANES - 1)
+        push = jnp.where(by_far, far_push, noted_push[k])
+        push = jnp.where(place_in == (4, 3)[k], push, own_pushes[k])
+        strip_after.append(ring_step(moved[k][4], strip_speed[k], push - strip_force[k]))
+
+    low, high = (place_in == 4) | (place_in == 5), (place_in == 2) | (place_in == 3)
+    edge_now = jnp.where(low, strip_after[0][0], jnp.where(high, strip_after[1][0], known))
+    edge_fast = jnp.where(place_in == 5, strip_after[0][1], jnp.where(place_in == 2, strip_after[1][1], known_fast))
+    (edge_force,) = side_forces([[roll(edge_now, -(GROUP * di + dj)) for di in (-1, 0, 1) for dj in (-1, 0, 1)]])
+    at_point = jnp.where(surface, known_point + edge_now, known_point)
+    past = edge_fast + known_gain * (push_of(known_facet, at_point) - edge_force)
+    moved_to = edge_now + TIME_STEP * past
+    side = (lane < 2) | (lane >= LANES - 2)
     for i in range(ROWS):
-        mid = rows[i][1]
-        at_point = of_row(base, i)
-        at_point = jnp.where(surface, at_point + mid, at_point)
-        net = push_of(later[i], at_point) - force[i]
-        past = jnp.where(side, (mid - here[i]) * (1.0 / TIME_STEP), fast[i])
-        past = past + gain[i] * net
-        out_vel[pl.ds(i, 6, stride=8), :] = past[0:6]
-        out_disp[pl.ds(i, 6, stride=8), :] = (mid + TIME_STEP * past)[0:6]
+        for ref, x in ((out_vel, past), (out_disp, moved_to)):
+            fixed = jnp.where(lane < 2, roll(x, -(GROUP * i + 5)), roll(x, LANES - 3 - GROUP * i))
+            at_row = pl.ds(i, 6, stride=8)
+            ref[at_row, :] = jnp.where(side[0:6], fixed[0:6], ref[at_row, :])
 
     landed(planar, 0).wait()
 
@@ -519,6 +592,8 @@
             pltpu.VMEM((2, 32, LANES), F32),
             pltpu.VMEM((2, 8, LANES), F32),
             pltpu.VMEM((2, 2, 8, LANES), F32),
+            pltpu.VMEM((8 * len(SPREAD), LANES), F32),
+            pltpu.VMEM((2 * 9 * 8, LANES), F32),
             dma((9,)),
             pltpu.SemaphoreType.REGULAR,
         ],

time: 11 us -> 10.8 us (0.982)
  Pallas kernels: 10.2 us -> 10 us
    pallas_call x1, Pallas kernels: 9.51 us -> 9.36 us  [shards(): pl.pallas_call(functools.partial(kernel, n_mesh, n_sub, width), out_shape...]
where the time goes in v5:
time: 10.8 us; the launch traced here: 10.6 us
  Pallas kernels  10 us (93%)
  between operations  0.64 us (6%)
    pallas_call x1, Pallas kernels, shards(): pl.pallas_call(functools.partial(kernel, n_mesh, n_sub, width), out_shape...  9.36 us
    pallas_call x1, Pallas kernels, shards(): pl.pallas_call(flush, out_shape=[jax.ShapeDtypeStruct((6 * ROWS, LANES),...  0.64 us

profile of v5, /device:TPU:0, one launch (start us, length us, event | category | flops | bytes accessed | tf_op | source)
XLA Modules:
  0.0 10.6 jit_solution(13600903465247961019)
XLA Ops:
  0.6 9.4 %shard_map.113 = (f32[48,128]{1,0:T(8,128)S(1)}, f32[48,128]{1,0:T(8,128)S(1)}) custom-call(f32[24,24]{1,0:T(8,128)} %stiff_hbm.1, s32[2,8]{1,0:T(2,128)} %bitcast.19, f32[48,128]{1,0:T(8,128)} %bitcast.11, f32[48,128]{1,0:T(8,128)} %bitcast.12, f32[16,128]{1,0:T(8,128)} %bitcast.15, f32[16,128]{1,0:T(8,128)} %bitcast.16, f32[24,128]{1,0:T(8,128)} %bitcast.14, ...), custom_call_target="tpu_custom_call" | custom-call | tf_op jit(solution)/shard_map/pallas_call | solution.py:575
  10.0 0.6 %shard_map.114 = (f32[48,128]{1,0:T(8,128)}, f32[48,128]{1,0:T(8,128)}) custom-call(f32[48,128]{1,0:T(8,128)S(1)} %get-tuple-element.6.moved, f32[48,128]{1,0:T(8,128)S(1)} %get-tuple-element.7.speed), custom_call_target="tpu_custom_call" | custom-call | tf_op jit(solution)/shard_map/pallas_call | solution.py:613

commit v6 on v5

--- a/solution.py
+++ b/solution.py
@@ -149,6 +149,8 @@
     copies = [
         pltpu.make_async_copy(src, dst, sems.at[i])
         for src, dst, i in [
+            (facets_hbm, raw.at[pl.ds(0, 6 * chunks)], 2),
+            (penalty_hbm, raw.at[pl.ds(6 * chunks, chunks)], 2),
             (disp_hbm, own.at[pl.ds(0, 48)], 0),
             (moduli_hbm, own.at[pl.ds(48, 16)], 0),
             (owners_hbm, owners, 1),
@@ -157,11 +159,6 @@
             (mass_hbm, mass, 0),
         ]
         + [(surf_hbm.at[pl.ds(8 * m, 8)], base.at[pl.ds(16 * m, 8)], 0) for m in range(3)]
-        + [
-            (facets_hbm, raw.at[pl.ds(0, 6 * chunks)], 2),
-            (penalty_hbm, raw.at[pl.ds(6 * chunks, chunks)], 2),
-            (stiff_hbm, stiff, 3),
-        ]
     ]
     for copy in copies:
         copy.start()
@@ -206,33 +203,6 @@
         base[pl.ds(8 * p, 8), :] = flat
     base[pl.ds(48, 8), :] = flat - 1.0
 
-    landed(152 + 16, 0).wait()
-    copies[2].wait()
-
-    holder = jnp.zeros((8, LANES), jnp.int32)
-    for b in range(ROWS):
-        holder = jnp.where(plane == b, owners[0, b], holder)
-    base[pl.ds(56, 8), :] = ((holder << bits) + pairs[pl.ds(0, 8), :]).astype(F32)
-
-    def of_row(ref, i):
-        return ref[pl.ds(i, 8, stride=8), :]
-
-    here = {i: of_row(own, i) for i in range(ROWS)}
-    speed = {i: of_row(vel, i) for i in range(ROWS)}
-    point = {i: of_row(base, i) for i in range(ROWS)}
-    point = {i: jnp.where(surface, point[i] + here[i], point[i]) for i in range(ROWS)}
-
-    sent = flat
-    for g, i in [(i, i) for i in range(ROWS)] + [(8, 0), (9, 1), (14, 6), (15, 7)]:
-        deep = roll(here[i], GROUP * g + 4)
-        deep = jnp.where(place_in < 2, roll(point[i], GROUP * g + 1), deep)
-        deep = jnp.where(place_in > 5, roll(speed[i], GROUP * g + 7), deep)
-        sent = jnp.where(group == g, deep, sent)
-    edge[...] = sent
-    for k, ids in enumerate(((6, 7, 7, 7), (0, 1, 0, 0))):
-        for j, (what, i) in enumerate(zip((here, here, speed, point), ids)):
-            border[k, pl.ds(8 * j, 8), :] = what[i]
-
     landed(7 * chunks, 2).wait()
     parts = [raw[pl.ds(chunks * c, chunks), :] for c in range(7)]
     root = jnp.sqrt(parts[6])
@@ -243,8 +213,6 @@
             tables[q, pl.ds(2 * c + h, half, stride=8), :] = values[half * h : half * (h + 1)]
 
     expected = n_mesh - 1 + jnp.where(first, 1, jnp.where(odd, jnp.where(last, n_mesh + 1, 2), n_mesh + 1))
-    pl.semaphore_wait(barrier, expected)
-
     def send(source, target, device, going, coming):
         return pltpu.make_async_remote_copy(
             src_ref=source,
@@ -255,15 +223,53 @@
             device_id_type=MESH,
         )
 
+    def send_table(ds, t):
+        place = pl.ds(pl.multiple_of(q * size, size), size)
+        send(tables.at[q], distant.at[place], (t, lax.rem(s + ds + n_sub, n_sub)), 2, 4).start()
+
+    @pl.when(last)
+    def _():
+        pl.semaphore_wait(barrier, expected)
+        send_table(1, 0)
+
+    landed(152 + 16, 0).wait()
+    copies[4].wait()
+    stiff_copy = pltpu.make_async_copy(stiff_hbm, stiff, sems.at[1])
+    stiff_copy.start()
+
+    holder = jnp.zeros((8, LANES), jnp.int32)
+    for b in range(ROWS):
+        holder = jnp.where(plane == b, owners[0, b], holder)
+    base[pl.ds(56, 8), :] = ((holder << bits) + pairs[pl.ds(0, 8), :]).astype(F32)
+
+    def of_row(ref, i):
+        return ref[pl.ds(i, 8, stride=8), :]
+
+    here = {i: of_row(own, i) for i in range(ROWS)}
+    speed = {i: of_row(vel, i) for i in range(ROWS)}
+    point = {i: of_row(base, i) for i in range(ROWS)}
+    point = {i: jnp.where(surface, point[i] + here[i], point[i]) for i in range(ROWS)}
+
+    sent = flat
+    for g, i in [(i, i) for i in range(ROWS)] + [(8, 0), (9, 1), (14, 6), (15, 7)]:
+        deep = roll(here[i], GROUP * g + 4)
+        deep = jnp.where(place_in == 0, roll(point[i], GROUP * g + 1), deep)
+        deep = jnp.where(place_in == 7, roll(point[i], GROUP * g + 7), deep)
+        deep = jnp.where(place_in == 1, roll(speed[i], GROUP * g + 2), deep)
+        deep = jnp.where(place_in == 6, roll(speed[i], GROUP * g + 6), deep)
+        sent = jnp.where(group == g, deep, sent)
+    edge[...] = sent
+    for k, ids in enumerate(((6, 7, 7, 7), (0, 1, 0, 0))):
+        for j, (what, i) in enumerate(zip((here, here, speed, point), ids)):
+            border[k, pl.ds(8 * j, 8), :] = what[i]
+
+    @pl.when(jnp.logical_not(last))
+    def _():
+        pl.semaphore_wait(barrier, expected)
+
     def send_direct(ds):
-        place = pl.multiple_of(q * size, size)
-
-        def to(t):
-            device = (t, lax.rem(s + ds + n_sub, n_sub))
-            send(tables.at[q], distant.at[pl.ds(place, size)], device, 1, 8).start()
-
         def edge_to(dq):
-            send(edge, edges.at[2 - dq], at(dq, ds), 1, 7).start()
+            send(edge, edges.at[2 - dq], at(dq, ds), 2, 4).start()
 
         for dq in (0, 1, -1):
 
@@ -271,7 +277,8 @@
             def _():
                 edge_to(dq)
 
-        to(0)
+        if ds == -1:
+            send_table(ds, 0)
         for dq in (0, 1, -1):
 
             @pl.when(at(dq, 0)[0] != 0)
@@ -279,7 +286,7 @@
                 edge_to(dq)
 
         for t in range(1, n_mesh):
-            to(t)
+            send_table(ds, t)
 
     @pl.when(last)
     def _():
@@ -291,12 +298,12 @@
 
             @pl.when(lax.rem(q + dq + n_mesh, n_mesh) == t)
             def _():
-                send(border.at[k], borders.at[k], (t, s), 0, 4).start()
-                send(edge, edges.at[4 * k], (t, s), 0, 4).start()
+                send(border.at[k], borders.at[k], (t, s), 0, 3).start()
+                send(edge, edges.at[4 * k], (t, s), 0, 3).start()
 
         @pl.when(q != t)
         def _():
-            send(tables.at[q], tables.at[q], (t, s), 0, 5).start()
+            send(tables.at[q], tables.at[q], (t, s), 0, 3).start()
 
     @pl.when(to_below)
     def _():
@@ -307,7 +314,7 @@
         for p in range(a, 8, 2):
             inverse[pl.ds(8 * p, 8), :] = slowness
     gain = {i: of_row(inverse, i) for i in range(ROWS)}
-    copies[11].wait()
+    stiff_copy.wait()
     weights, single = coefficients(stiff[...])
     for n, (off, p, g) in enumerate(SPREAD):
         column_of = single[8 * g : 8 * g + 8, 8 * off + p : 8 * off + p + 1]
@@ -408,7 +415,7 @@
     force = {}
     for i in (1, 3, 5):
         force[i], force[i + 1] = elastic(around(rows, i), around(rows, i + 1))
-    landed(2 * 8 + 2 * 32, 4).wait()
+    landed(planar, 3).wait()
     for i, (k, j) in {-2: (0, 0), -1: (0, 1), 8: (1, 0), 9: (1, 1)}.items():
         here[i] = borders[k, pl.ds(8 * j, 8), :]
         rows[i] = turned(here[i])
@@ -419,25 +426,23 @@
         return jnp.where(group < 8, middle, jnp.where(group < 12, behind, before))
 
     centre = column(sent, edges[0], edges[4])
-    landed((n_mesh - 1) * size, 5).wait()
-    own_point = roll(centre, 3)
-    own_push = push_of(facet_by(wanted_by(own_point), of_plane), own_point)
+    own_push = push_of(facet_by(wanted_by(centre), of_plane), centre)
 
     note[0] = centre
     note[1] = own_push
 
     @pl.when(jnp.logical_not(last))
     def _():
-        send(note, noted.at[0], at(0, 1), 2, 6).start()
+        send(note, noted.at[0], at(0, 1), 1, 4).start()
 
     @pl.when(odd)
     def _():
-        send(note, noted.at[1], at(0, -1), 3, 6).start()
+        send(note, noted.at[1], at(0, -1), 1, 4).start()
 
     @pl.when(first)
     def _():
         pl.semaphore_wait(ready, 1)
-        send(note, noted.at[1], at(0, -1), 3, 6).start()
+        send(note, noted.at[1], at(0, -1), 1, 4).start()
 
     later = {}
     after, fast = {}, {}
@@ -465,55 +470,51 @@
         made = flat
         for i in indices:
             g = i % GROUPS
-            piece = jnp.where(place_in < 4, roll(rows_of[i], GROUP * g + 3), roll(rows_of[i], GROUP * g + 5))
+            piece = jnp.where(place_in < 4, roll(rows_of[i], GROUP * g + 1), roll(rows_of[i], GROUP * g + 7))
             made = jnp.where(group == g, piece, made)
         return made
 
     known = strip_of(after, range(-1, 9))
     known_fast, known_gain, known_facet = (strip_of(x, range(ROWS)) for x in (fast, gain, later))
     known_point = strip_of({i: of_row(base, i) for i in range(ROWS)}, range(ROWS))
-    shifts = (1, -1)
-    own_pushes = [roll(own_push, shift) for shift in shifts]
+    shifts = (-3, 3)
+    own_pushes = [roll(own_push, -6), roll(own_push, 6)]
 
     has_direct = from_last | from_above
 
     @pl.when(jnp.logical_not(has_direct))
     def _():
-        landed(2 * 2 * 8, 6).wait()
+        landed(2 * 2 * 8, 4).wait()
 
     @pl.when(has_direct)
     def _():
-        landed(2 * 8, 6).wait()
-        landed(3 * 8, 7).wait()
+        landed(2 * 8 + direct, 4).wait()
 
     far = column(edges[2], edges[1], edges[3])
     left, right = jnp.where(from_last, far, noted[0, 0]), jnp.where(from_above, far, noted[1, 0])
-    from_before = (place_in == 0) | (place_in == 2) | (place_in == 3) | (place_in == 6)
+    from_before = place_in < 4
     strips = [jnp.where(from_before, left, centre), jnp.where(from_before, centre, right)]
     moved = [
         [roll(x, shift - (GROUP * di + dj)) for di in (-1, 0, 1) for dj in (-1, 0, 1)]
         for x, shift in zip(strips, shifts)
     ]
     strip_force = side_forces(moved)
-    strip_speed = [roll(x, shift - 3) for x, shift in zip(strips, shifts)]
-    far_point = jnp.where(from_last, roll(far, 3 + shifts[0]), roll(far, 3 + shifts[1]))
-    far_wanted = wanted_by(far_point)
-    noted_push = [roll(noted[k, 1], shifts[k]) for k in range(2)]
-
-    @pl.when(has_direct)
-    def _():
-        landed(n_mesh * size, 8).wait()
-
-    far_push = push_of(facet_by(far_wanted, of_side), far_point)
+    strip_speed = [
+        jnp.where(place_in == 0, roll(strips[0], -1), roll(strips[0], -5)),
+        jnp.where(place_in == 7, roll(strips[1], 1), roll(strips[1], 5)),
+    ]
+    far_wanted = wanted_by(far)
+
+    far_push = push_of(facet_by(far_wanted, of_side), far)
     strip_after = []
     for k, by_far in enumerate((from_last, from_above)):
-        push = jnp.where(by_far, far_push, noted_push[k])
-        push = jnp.where(place_in == (4, 3)[k], push, own_pushes[k])
+        push = jnp.where(by_far, far_push, noted[k, 1])
+        push = jnp.where(place_in == (0, 7)[k], push, own_pushes[k])
         strip_after.append(ring_step(moved[k][4], strip_speed[k], push - strip_force[k]))
 
-    low, high = (place_in == 4) | (place_in == 5), (place_in == 2) | (place_in == 3)
+    low, high = place_in < 2, place_in > 5
     edge_now = jnp.where(low, strip_after[0][0], jnp.where(high, strip_after[1][0], known))
-    edge_fast = jnp.where(place_in == 5, strip_after[0][1], jnp.where(place_in == 2, strip_after[1][1], known_fast))
+    edge_fast = jnp.where(place_in == 1, strip_after[0][1], jnp.where(place_in == 6, strip_after[1][1], known_fast))
     (edge_force,) = side_forces([[roll(edge_now, -(GROUP * di + dj)) for di in (-1, 0, 1) for dj in (-1, 0, 1)]])
     at_point = jnp.where(surface, known_point + edge_now, known_point)
     past = edge_fast + known_gain * (push_of(known_facet, at_point) - edge_force)
@@ -521,7 +522,7 @@
     side = (lane < 2) | (lane >= LANES - 2)
     for i in range(ROWS):
         for ref, x in ((out_vel, past), (out_disp, moved_to)):
-            fixed = jnp.where(lane < 2, roll(x, -(GROUP * i + 5)), roll(x, LANES - 3 - GROUP * i))
+            fixed = jnp.where(lane < 2, roll(x, -(GROUP * i + 1)), roll(x, LANES - 7 - GROUP * i))
             at_row = pl.ds(i, 6, stride=8)
             ref[at_row, :] = jnp.where(side[0:6], fixed[0:6], ref[at_row, :])
 
@@ -529,15 +530,17 @@
 
     @pl.when(to_below | last)
     def _():
-        landed(direct, 1).wait()
-
-    @pl.when(jnp.logical_not(last))
-    def _():
-        landed(2 * 8, 2).wait()
-
-    @pl.when(odd | first)
-    def _():
-        landed(2 * 8, 3).wait()
+        landed(direct, 2).wait()
+
+    two_notes = first | (odd & jnp.logical_not(last))
+
+    @pl.when(two_notes)
+    def _():
+        landed(2 * 2 * 8, 1).wait()
+
+    @pl.when(jnp.logical_not(two_notes))
+    def _():
+        landed(2 * 8, 1).wait()
 
 
 def flush(moved, speed, out_moved, out_speed, sem):
@@ -594,7 +597,7 @@
             pltpu.VMEM((2, 2, 8, LANES), F32),
             pltpu.VMEM((8 * len(SPREAD), LANES), F32),
             pltpu.VMEM((2 * 9 * 8, LANES), F32),
-            dma((9,)),
+            dma((5,)),
             pltpu.SemaphoreType.REGULAR,
         ],
         compiler_params=pltpu.CompilerParams(collective_id=0, has_side_effects=True),

time: 10.8 us -> 10.7 us (level)
  Pallas kernels: 10 us -> 9.86 us
    pallas_call x1, Pallas kernels: 9.36 us -> 9.22 us  [shards(): pl.pallas_call(functools.partial(kernel, n_mesh, n_sub, width), out_shape...]
where the time goes in v6:
time: 10.7 us; the launch traced here: 10.5 us
  Pallas kernels  9.86 us (92%)
  between operations  0.64 us (6%)
    pallas_call x1, Pallas kernels, shards(): pl.pallas_call(functools.partial(kernel, n_mesh, n_sub, width), out_shape...  9.22 us
    pallas_call x1, Pallas kernels, shards(): pl.pallas_call(flush, out_shape=[jax.ShapeDtypeStruct((6 * ROWS, LANES),...  0.64 us

profile of v6, /device:TPU:0, one launch (start us, length us, event | category | flops | bytes accessed | tf_op | source)
XLA Modules:
  0.0 10.5 jit_solution(16406846892011377123)
XLA Ops:
  0.6 9.2 %shard_map.113 = (f32[48,128]{1,0:T(8,128)S(1)}, f32[48,128]{1,0:T(8,128)S(1)}) custom-call(f32[24,24]{1,0:T(8,128)} %stiff_hbm.1, s32[2,8]{1,0:T(2,128)} %bitcast.19, f32[48,128]{1,0:T(8,128)} %bitcast.11, f32[48,128]{1,0:T(8,128)} %bitcast.12, f32[16,128]{1,0:T(8,128)} %bitcast.15, f32[16,128]{1,0:T(8,128)} %bitcast.16, f32[24,128]{1,0:T(8,128)} %bitcast.14, ...), custom_call_target="tpu_custom_call" | custom-call | tf_op jit(solution)/shard_map/pallas_call | solution.py:578
  9.9 0.6 %shard_map.114 = (f32[48,128]{1,0:T(8,128)}, f32[48,128]{1,0:T(8,128)}) custom-call(f32[48,128]{1,0:T(8,128)S(1)} %get-tuple-element.6.moved, f32[48,128]{1,0:T(8,128)S(1)} %get-tuple-element.7.speed), custom_call_target="tpu_custom_call" | custom-call | tf_op jit(solution)/shard_map/pallas_call | solution.py:616

commit v7 on v6

--- a/solution.py
+++ b/solution.py
@@ -225,7 +225,7 @@
 
     def send_table(ds, t):
         place = pl.ds(pl.multiple_of(q * size, size), size)
-        send(tables.at[q], distant.at[place], (t, lax.rem(s + ds + n_sub, n_sub)), 2, 4).start()
+        send(tables.at[q], distant.at[place], (t, lax.rem(s + ds + n_sub, n_sub)), 2, 5 if ds == 1 else 4).start()
 
     @pl.when(last)
     def _():
@@ -237,18 +237,15 @@
     stiff_copy = pltpu.make_async_copy(stiff_hbm, stiff, sems.at[1])
     stiff_copy.start()
 
-    holder = jnp.zeros((8, LANES), jnp.int32)
-    for b in range(ROWS):
-        holder = jnp.where(plane == b, owners[0, b], holder)
-    base[pl.ds(56, 8), :] = ((holder << bits) + pairs[pl.ds(0, 8), :]).astype(F32)
-
     def of_row(ref, i):
         return ref[pl.ds(i, 8, stride=8), :]
 
     here = {i: of_row(own, i) for i in range(ROWS)}
     speed = {i: of_row(vel, i) for i in range(ROWS)}
     point = {i: of_row(base, i) for i in range(ROWS)}
-    point = {i: jnp.where(surface, point[i] + here[i], point[i]) for i in range(ROWS)}
+    for i in range(ROWS):
+        code = jnp.broadcast_to(pairs[pl.ds(i, 1), :] + (owners[0, i] << bits), (8, LANES)).astype(F32)
+        point[i] = jnp.where(surface, point[i] + here[i], jnp.where(plane == 7, code, point[i]))
 
     sent = flat
     for g, i in [(i, i) for i in range(ROWS)] + [(8, 0), (9, 1), (14, 6), (15, 7)]:
@@ -269,7 +266,7 @@
 
     def send_direct(ds):
         def edge_to(dq):
-            send(edge, edges.at[2 - dq], at(dq, ds), 2, 4).start()
+            send(edge, edges.at[2 - dq + (4 if ds == 1 else 0)], at(dq, ds), 2, 5 if ds == 1 else 4).start()
 
         for dq in (0, 1, -1):
 
@@ -480,25 +477,37 @@
     shifts = (-3, 3)
     own_pushes = [roll(own_push, -6), roll(own_push, 6)]
 
-    has_direct = from_last | from_above
-
-    @pl.when(jnp.logical_not(has_direct))
+    @pl.when(from_above)
+    def _():
+        landed(2 * 8 + direct, 4).wait()
+
+    @pl.when(first)
+    def _():
+        landed(2 * 8, 4).wait()
+
+    @pl.when(jnp.logical_not(first | from_above))
     def _():
         landed(2 * 2 * 8, 4).wait()
 
-    @pl.when(has_direct)
-    def _():
-        landed(2 * 8 + direct, 4).wait()
-
-    far = column(edges[2], edges[1], edges[3])
-    left, right = jnp.where(from_last, far, noted[0, 0]), jnp.where(from_above, far, noted[1, 0])
+    above = column(edges[2], edges[1], edges[3])
+
+    def turned_strip(x, shift):
+        return [roll(x, shift - (GROUP * di + dj)) for di in (-1, 0, 1) for dj in (-1, 0, 1)]
+
     from_before = place_in < 4
-    strips = [jnp.where(from_before, left, centre), jnp.where(from_before, centre, right)]
-    moved = [
-        [roll(x, shift - (GROUP * di + dj)) for di in (-1, 0, 1) for dj in (-1, 0, 1)]
-        for x, shift in zip(strips, shifts)
-    ]
-    strip_force = side_forces(moved)
+    right = jnp.where(from_before, centre, jnp.where(from_above, above, noted[1, 0]))
+    moved_right = turned_strip(right, shifts[1])
+    (force_right,) = side_forces([moved_right])
+
+    @pl.when(first)
+    def _():
+        landed(direct, 5).wait()
+
+    far = jnp.where(first, column(edges[6], edges[5], edges[7]), above)
+    left = jnp.where(from_before, jnp.where(from_last, far, noted[0, 0]), centre)
+    moved_left = turned_strip(left, shifts[0])
+    (force_left,) = side_forces([moved_left])
+    strips, moved, strip_force = (left, right), (moved_left, moved_right), (force_left, force_right)
     strip_speed = [
         jnp.where(place_in == 0, roll(strips[0], -1), roll(strips[0], -5)),
         jnp.where(place_in == 7, roll(strips[1], 1), roll(strips[1], 5)),
@@ -591,13 +600,13 @@
             pltpu.VMEM((n_mesh * 4 * width // LANES + 128, LANES), F32),
             pltpu.VMEM((8, LANES), F32),
             pltpu.VMEM((2, 32, LANES), F32),
-            pltpu.VMEM((5, 8, LANES), F32),
+            pltpu.VMEM((8, 8, LANES), F32),
             pltpu.VMEM((2, 32, LANES), F32),
             pltpu.VMEM((2, 8, LANES), F32),
             pltpu.VMEM((2, 2, 8, LANES), F32),
             pltpu.VMEM((8 * len(SPREAD), LANES), F32),
             pltpu.VMEM((2 * 9 * 8, LANES), F32),
-            dma((5,)),
+            dma((6,)),
             pltpu.SemaphoreType.REGULAR,
         ],
         compiler_params=pltpu.CompilerParams(collective_id=0, has_side_effects=True),

time: 10.7 us -> 10.7 us (level)
  no operation moved by 1% of the time
where the time goes in v7:
time: 10.7 us; the launch traced here: 10.5 us
  Pallas kernels  9.83 us (92%)
  between operations  0.64 us (6%)
    pallas_call x1, Pallas kernels, shards(): pl.pallas_call(functools.partial(kernel, n_mesh, n_sub, width), out_shape...  9.19 us
    pallas_call x1, Pallas kernels, shards(): pl.pallas_call(flush, out_shape=[jax.ShapeDtypeStruct((6 * ROWS, LANES),...  0.64 us

profile of v7, /device:TPU:0, one launch (start us, length us, event | category | flops | bytes accessed | tf_op | source)
XLA Modules:
  0.0 10.5 jit_solution(10457376085468618026)
XLA Ops:
  0.6 9.2 %shard_map.113 = (f32[48,128]{1,0:T(8,128)S(1)}, f32[48,128]{1,0:T(8,128)S(1)}) custom-call(f32[24,24]{1,0:T(8,128)} %stiff_hbm.1, s32[2,8]{1,0:T(2,128)} %bitcast.19, f32[48,128]{1,0:T(8,128)} %bitcast.11, f32[48,128]{1,0:T(8,128)} %bitcast.12, f32[16,128]{1,0:T(8,128)} %bitcast.15, f32[16,128]{1,0:T(8,128)} %bitcast.16, f32[24,128]{1,0:T(8,128)} %bitcast.14, ...), custom_call_target="tpu_custom_call" | custom-call | tf_op jit(solution)/shard_map/pallas_call | solution.py:587
  9.8 0.6 %shard_map.114 = (f32[48,128]{1,0:T(8,128)}, f32[48,128]{1,0:T(8,128)}) custom-call(f32[48,128]{1,0:T(8,128)S(1)} %get-tuple-element.6.moved, f32[48,128]{1,0:T(8,128)S(1)} %get-tuple-element.7.speed), custom_call_target="tpu_custom_call" | custom-call | tf_op jit(solution)/shard_map/pallas_call | solution.py:625

commit v8 on v6

--- a/solution.py
+++ b/solution.py
@@ -237,18 +237,15 @@
     stiff_copy = pltpu.make_async_copy(stiff_hbm, stiff, sems.at[1])
     stiff_copy.start()
 
-    holder = jnp.zeros((8, LANES), jnp.int32)
-    for b in range(ROWS):
-        holder = jnp.where(plane == b, owners[0, b], holder)
-    base[pl.ds(56, 8), :] = ((holder << bits) + pairs[pl.ds(0, 8), :]).astype(F32)
-
     def of_row(ref, i):
         return ref[pl.ds(i, 8, stride=8), :]
 
     here = {i: of_row(own, i) for i in range(ROWS)}
     speed = {i: of_row(vel, i) for i in range(ROWS)}
     point = {i: of_row(base, i) for i in range(ROWS)}
-    point = {i: jnp.where(surface, point[i] + here[i], point[i]) for i in range(ROWS)}
+    for i in range(ROWS):
+        code = jnp.broadcast_to(pairs[pl.ds(i, 1), :] + (owners[0, i] << bits), (8, LANES)).astype(F32)
+        point[i] = jnp.where(surface, point[i] + here[i], jnp.where(plane == 7, code, point[i]))
 
     sent = flat
     for g, i in [(i, i) for i in range(ROWS)] + [(8, 0), (9, 1), (14, 6), (15, 7)]:

time: 10.7 us -> 10.7 us (level)
  no operation moved by 1% of the time
where the time goes in v8:
time: 10.7 us; the launch traced here: 10.5 us
  Pallas kernels  9.85 us (92%)
  between operations  0.64 us (6%)
    pallas_call x1, Pallas kernels, shards(): pl.pallas_call(functools.partial(kernel, n_mesh, n_sub, width), out_shape...  9.22 us
    pallas_call x1, Pallas kernels, shards(): pl.pallas_call(flush, out_shape=[jax.ShapeDtypeStruct((6 * ROWS, LANES),...  0.64 us

profile of v8, /device:TPU:0, one launch (start us, length us, event | category | flops | bytes accessed | tf_op | source)
XLA Modules:
  0.0 10.5 jit_solution(9226767500772700313)
XLA Ops:
  0.6 9.2 %shard_map.113 = (f32[48,128]{1,0:T(8,128)S(1)}, f32[48,128]{1,0:T(8,128)S(1)}) custom-call(f32[24,24]{1,0:T(8,128)} %stiff_hbm.1, s32[2,8]{1,0:T(2,128)} %bitcast.19, f32[48,128]{1,0:T(8,128)} %bitcast.11, f32[48,128]{1,0:T(8,128)} %bitcast.12, f32[16,128]{1,0:T(8,128)} %bitcast.15, f32[16,128]{1,0:T(8,128)} %bitcast.16, f32[24,128]{1,0:T(8,128)} %bitcast.14, ...), custom_call_target="tpu_custom_call" | custom-call | tf_op jit(solution)/shard_map/pallas_call | solution.py:575
  9.9 0.6 %shard_map.114 = (f32[48,128]{1,0:T(8,128)}, f32[48,128]{1,0:T(8,128)}) custom-call(f32[48,128]{1,0:T(8,128)S(1)} %get-tuple-element.6.moved, f32[48,128]{1,0:T(8,128)S(1)} %get-tuple-element.7.speed), custom_call_target="tpu_custom_call" | custom-call | tf_op jit(solution)/shard_map/pallas_call | solution.py:613
